TPU v7x, 32 devices: a whole 2x2x4 slice. The times are simulated.
32 devices in a mesh: dp: 8 (over z, core), tensor: 4 (over y, x).
Axes of the slice: x: 2, y: 2, z: 4, core: 2. Of those that a mesh axis runs over, the one named last changes fastest.
Arguments:
- hidden: bfloat16 [2048, 8, 1536], P('tensor', 'dp'), may hold values from -6 to 6
- cotangent: bfloat16 [2048, 8, 1536], P('tensor', 'dp'), may hold values from -6 to 6
- input_gain: float32 [1536], replicated, may hold values from 0.5 to 1.5
- inner_weight: float32 [2, 1536, 3072], P(None, 'dp', 'tensor'), may hold values from -0.15625 to 0.15625
- step_weight: float32 [1536, 48], P('dp', 'tensor'), may hold values from -0.15625 to 0.15625
- state_weight: float32 [1536, 256], P(('dp', 'tensor')), may hold values from -0.15625 to 0.15625
- inner_taps: float32 [5, 3072], P(None, 'tensor'), may hold values from -3 to 3
- state_taps: float32 [5, 256], replicated, may hold values from -3 to 3
- head_params: float32 [3, 48], P(None, 'tensor'), may hold values from -7 to 3, as said below
- gated_gain: float32 [3072], P('tensor'), may hold values from 0.5 to 1.5
- output_matrix: float32 [3072, 1536], P('tensor', 'dp'), may hold values from -0.109375 to 0.109375
- first_input_gain: float32 [1536], replicated, may hold values from -6 to 6
- first_inner_weight: float32 [2, 1536, 3072], P(None, 'dp', 'tensor'), may hold values from -6 to 6
- first_step_weight: float32 [1536, 48], P('dp', 'tensor'), may hold values from -6 to 6
- first_state_weight: float32 [1536, 256], P(('dp', 'tensor')), may hold values from -6 to 6
- first_inner_taps: float32 [5, 3072], P(None, 'tensor'), may hold values from -6 to 6
- first_state_taps: float32 [5, 256], replicated, may hold values from -6 to 6
- first_head_params: float32 [3, 48], P(None, 'tensor'), may hold values from -6 to 6
- first_gated_gain: float32 [3072], P('tensor'), may hold values from -6 to 6
- first_output_weight: float32 [3072, 1536], P('tensor', 'dp'), may hold values from -6 to 6
- second_input_gain: float32 [1536], replicated, may hold values from 1 to 163
- second_inner_weight: float32 [2, 1536, 3072], P(None, 'dp', 'tensor'), may hold values from 1 to 163
- second_step_weight: float32 [1536, 48], P('dp', 'tensor'), may hold values from 1 to 163
- second_state_weight: float32 [1536, 256], P(('dp', 'tensor')), may hold values from 1 to 163
- second_inner_taps: float32 [5, 3072], P(None, 'tensor'), may hold values from 1 to 163
- second_state_taps: float32 [5, 256], replicated, may hold values from 1 to 163
- second_head_params: float32 [3, 48], P(None, 'tensor'), may hold values from 1 to 163
- second_gated_gain: float32 [3072], P('tensor'), may hold values from 1 to 163
- second_output_weight: float32 [3072, 1536], P('tensor', 'dp'), may hold values from 1 to 163
Outputs:
- result: bfloat16 [2048, 8, 1536], P('tensor', 'dp')
- gradient_hidden: float32 [2048, 8, 1536], P('tensor', 'dp')
- gradient_input_gain: float32 [1536], replicated
- gradient_inner_weight: float32 [2, 1536, 3072], P(None, 'dp', 'tensor')
- step_weight_gradient: float32 [1536, 48], P('dp', 'tensor')
- gradient_state_weight: float32 [1536, 256], P(('dp', 'tensor'))
- gradient_inner_taps: float32 [5, 3072], P(None, 'tensor')
- gradient_state_taps: float32 [5, 256], replicated
- gradient_head_params: float32 [3, 48], P(None, 'tensor')
- gradient_gated_gain: float32 [3072], P('tensor')
- gradient_output_weight: float32 [3072, 1536], P('tensor', 'dp')
- updated_input_gain: float32 [1536], replicated
- updated_inner_weight: float32 [2, 1536, 3072], P(None, 'dp', 'tensor')
- updated_step_weight: float32 [1536, 48], P('dp', 'tensor')
- updated_state_weight: float32 [1536, 256], P(('dp', 'tensor'))
- updated_inner_taps: float32 [5, 3072], P(None, 'tensor')
- updated_state_taps: float32 [5, 256], replicated
- updated_head_params: float32 [3, 48], P(None, 'tensor')
- updated_gated_gain: float32 [3072], P('tensor')
- updated_output_weight: float32 [3072, 1536], P('tensor', 'dp')
- updated_first_input_gain: float32 [1536], replicated
- updated_first_inner_weight: float32 [2, 1536, 3072], P(None, 'dp', 'tensor')
- updated_first_step_weight: float32 [1536, 48], P('dp', 'tensor')
- updated_first_state_weight: float32 [1536, 256], P(('dp', 'tensor'))
- updated_first_inner_taps: float32 [5, 3072], P(None, 'tensor')
- updated_first_state_taps: float32 [5, 256], replicated
- updated_first_head_params: float32 [3, 48], P(None, 'tensor')
- updated_first_gated_gain: float32 [3072], P('tensor')
- updated_first_output_weight: float32 [3072, 1536], P('tensor', 'dp')
- updated_second_input_gain: float32 [1536], replicated
- updated_second_inner_weight: float32 [2, 1536, 3072], P(None, 'dp', 'tensor')
- updated_second_step_weight: float32 [1536, 48], P('dp', 'tensor')
- updated_second_state_weight: float32 [1536, 256], P(('dp', 'tensor'))
- updated_second_inner_taps: float32 [5, 3072], P(None, 'tensor')
- updated_second_state_taps: float32 [5, 256], replicated
- updated_second_head_params: float32 [3, 48], P(None, 'tensor')
- updated_second_gated_gain: float32 [3072], P('tensor')
- updated_second_output_weight: float32 [3072, 1536], P('tensor', 'dp')
Inputs may be any that keep to these rules, and one draw needn't show every extreme that they name: Row 0 of head_params lies in [-1, 2.8), row 1 in [-7, -2), row 2 in [0.5, 1.5).
All inputs are finite; a program needn't handle non-finite values.
Results may differ from a plain program's by a relative error of at most 0.01.
The roundings to bfloat16 on the way count: a program that leaves them out, or rounds other values in their place, can miss the bound.
Values may be sent and summed in bfloat16 or wider, within the bound.
A program may use at most 256 MiB of HBM per device.

v0:
```python
import jax
import jax.numpy as jnp
from jax import lax
from jax.sharding import PartitionSpec as P

GROUP = 256
INNER = 3072


norm_eps = 1e-05
beta_first = 0.9
beta_second = 0.95
adam_eps = 1e-08
decay_rate = 0.1
step_count = 4.0
rates = (0.2, 0.008, 0.008, 0.008, 0.1, 0.1, 0.4, 0.2, 0.006)
precise_setting = lax.Precision.HIGHEST


def contract_last(values, weight):
    return lax.dot_general(
        values, weight, (((1,), (1,)), ((), ())), preferred_element_type=jnp.float32
    )


def contract_first(left, right):
    return lax.dot_general(
        left, right, (((0,), (0,)), ((), ())), preferred_element_type=jnp.float32
    )


def conv_silu(values, taps):
    length = values.shape[0]
    width = taps.shape[0] - 1
    padded = jnp.pad(values, ((width - 1, 0), (0, 0), (0, 0)))
    total = jnp.broadcast_to(taps[width], values.shape)
    for offset in range(width):
        total = total + taps[offset] * padded[offset : offset + length]
    return jax.nn.silu(total)


def group_step(state, block):
    inputs, steps, logs, key_rows, query_rows = block
    cumul = jnp.cumsum(logs, axis=0)
    score_matrix = jnp.einsum("dtv,htv->dht", query_rows, key_rows, precision=precise_setting)
    count = logs.shape[0]
    causal = (jnp.arange(count)[:, None] >= jnp.arange(count)[None, :])[:, :, None, None]
    spread = jnp.where(causal, cumul[:, None] - cumul[None, :], 0.0)
    mixing = jnp.where(causal, jnp.exp(spread), 0.0) * score_matrix[..., None] * steps[None]
    inner_part = jnp.einsum("qksh,kshp->qshp", mixing, inputs, precision=precise_setting)
    carried = (
        jnp.einsum("qsn,shnp->qshp", query_rows, state, precision=precise_setting)
        * jnp.exp(cumul)[..., None]
    )
    final = cumul[-1]
    weights = jnp.exp(final[None] - cumul) * steps
    update = jnp.einsum(
        "ksn,kshp->shnp", key_rows, weights[..., None] * inputs, precision=precise_setting
    )
    return (jnp.exp(final)[..., None, None] * state + update, inner_part + carried)


def scan_heads(inputs, steps, logs, key_rows, query_rows):
    length, seqs, heads, size = inputs.shape
    blocks = length // GROUP

    def split(values):
        return values.reshape((blocks, GROUP) + values.shape[1:])

    start = jnp.zeros((seqs, heads, key_rows.shape[-1], size), jnp.float32)
    final_state, outputs = lax.scan(
        jax.checkpoint(group_step),
        start,
        (split(inputs), split(steps), split(logs), split(key_rows), split(query_rows)),
    )
    return outputs.reshape(inputs.shape)


def mixer(inner_pre, state_pre, step_pre, gate_pre, inner_taps, state_taps, head_params):
    length, seqs, width = inner_pre.shape
    heads = step_pre.shape[-1]
    half_state = state_pre.shape[-1] // 2
    inner_act = conv_silu(inner_pre, inner_taps).reshape(length, seqs, heads, width // heads)
    state_act = conv_silu(state_pre, state_taps)
    steps = jax.nn.softplus(step_pre + head_params[1])
    logs = -jnp.exp(head_params[0]) * steps
    scanned = scan_heads(
        inner_act, steps, logs, state_act[..., :half_state], state_act[..., half_state:]
    )
    mixed = scanned + head_params[2][:, None] * inner_act
    return mixed.reshape(length, seqs, width) * jax.nn.silu(gate_pre)


def adam_step(param, first, second_moment, grad, rate):
    first_new = beta_first * first + (1.0 - beta_first) * grad
    second_new = beta_second * second_moment + (1.0 - beta_second) * grad * grad
    first_hat = first_new / (1.0 - beta_first**step_count)
    second_hat = second_new / (1.0 - beta_second**step_count)
    moved = param - rate * (first_hat / (jnp.sqrt(second_hat) + adam_eps) + decay_rate * param)
    return (moved, first_new, second_new)


def body(
    hidden,
    cotangent,
    input_gain,
    inner_weight,
    step_weight,
    state_weight,
    inner_taps,
    state_taps,
    head_params,
    gated_gain,
    output_matrix,
    first_input_gain,
    first_inner_weight,
    first_step_weight,
    first_state_weight,
    first_inner_taps,
    first_state_taps,
    first_head_params,
    first_gated_gain,
    first_output_weight,
    second_input_gain,
    second_inner_weight,
    second_step_weight,
    second_state_weight,
    second_inner_taps,
    second_state_taps,
    second_head_params,
    second_gated_gain,
    second_output_weight,
):
    params = (
        input_gain,
        inner_weight,
        step_weight,
        state_weight,
        inner_taps,
        state_taps,
        head_params,
        gated_gain,
        output_matrix,
    )
    firsts = (
        first_input_gain,
        first_inner_weight,
        first_step_weight,
        first_state_weight,
        first_inner_taps,
        first_state_taps,
        first_head_params,
        first_gated_gain,
        first_output_weight,
    )
    seconds = (
        second_input_gain,
        second_inner_weight,
        second_step_weight,
        second_state_weight,
        second_inner_taps,
        second_state_taps,
        second_head_params,
        second_gated_gain,
        second_output_weight,
    )
    local_len, seqs, width = hidden.shape
    base = hidden.astype(jnp.float32)
    rstd = lax.rsqrt(jnp.mean(base * base, -1, keepdims=True) + norm_eps)
    normed = base * rstd
    normed_in = (normed * input_gain).astype(jnp.bfloat16)
    full_in, full_cot = (
        lax.all_gather(normed_in, "tensor", axis=0, tiled=True),
        lax.all_gather(cotangent, "tensor", axis=0, tiled=True),
    )
    inner_b, step_b, output_b = (
        lax.all_gather(inner_weight.astype(jnp.bfloat16), "dp", axis=1, tiled=True),
        lax.all_gather(step_weight.astype(jnp.bfloat16), "dp", axis=0, tiled=True),
        lax.all_gather(output_matrix.astype(jnp.bfloat16), "dp", axis=1, tiled=True),
    )
    state_b = lax.all_gather(
        state_weight.astype(jnp.bfloat16), ("dp", "tensor"), axis=0, tiled=True
    )
    length = full_in.shape[0]
    row_count = length * seqs
    flat_in = full_in.reshape(row_count, width)

    def project(weight):
        return jnp.dot(flat_in, weight, preferred_element_type=jnp.float32).reshape(
            length, seqs, weight.shape[1]
        )

    gate_pre = project(inner_b[0])
    inner_pre = project(inner_b[1])
    step_pre = project(step_b)
    state_pre = project(state_b)
    gated, pullback = jax.vjp(
        mixer, inner_pre, state_pre, step_pre, gate_pre, inner_taps, state_taps, head_params
    )
    total_squares = lax.psum(jnp.sum(gated * gated, -1), "tensor")
    scale = lax.rsqrt(total_squares[..., None] / INNER + norm_eps)
    unit = gated * scale
    local_inner = gated.shape[-1]
    normed_out = (unit * gated_gain).astype(jnp.bfloat16).reshape(row_count, local_inner)
    branch = lax.psum_scatter(
        jnp.dot(normed_out, output_b, preferred_element_type=jnp.float32),
        "tensor",
        scatter_dimension=0,
        tiled=True,
    ).reshape(local_len, seqs, width)
    result = (base + branch).astype(jnp.bfloat16)
    flat_cot = full_cot.reshape(row_count, width)
    d_normed = contract_last(flat_cot, output_b).reshape(length, seqs, local_inner)
    grad_output = contract_first(normed_out, flat_cot)
    grad_gated_gain = jnp.sum(d_normed * unit, (0, 1))
    d_unit = d_normed * gated_gain
    cross = lax.psum(jnp.sum(d_unit * unit, -1), "tensor")
    d_gated = scale * (d_unit - unit * (cross[..., None] / INNER))
    (
        d_inner_pre,
        d_state_pre,
        d_step_pre,
        d_gate_pre,
        grad_inner_taps,
        grad_state_taps,
        grad_head,
    ) = pullback(d_gated)

    def flatten(values):
        return values.reshape(row_count, values.shape[-1]).astype(jnp.bfloat16)

    gate_flat = flatten(d_gate_pre)
    inner_flat = flatten(d_inner_pre)
    step_flat = flatten(d_step_pre)
    state_flat = flatten(d_state_pre)
    grad_inner = jnp.stack(
        [contract_first(flat_in, gate_flat), contract_first(flat_in, inner_flat)]
    )
    grad_step = contract_first(flat_in, step_flat)
    grad_state = contract_first(flat_in, state_flat)

    def piece(values, weight):
        return contract_last(values, weight)

    d_in = lax.psum_scatter(
        piece(gate_flat, inner_b[0])
        + piece(inner_flat, inner_b[1])
        + piece(step_flat, step_b)
        + piece(state_flat, state_b),
        "tensor",
        scatter_dimension=0,
        tiled=True,
    ).reshape(local_len, seqs, width)
    grad_input_gain = jnp.sum(d_in * normed, (0, 1))
    d_hat = d_in * input_gain
    gradient_hidden = cotangent.astype(jnp.float32) + rstd * (
        d_hat - normed * jnp.mean(d_hat * normed, -1, keepdims=True)
    )
    summed = lax.psum(
        (grad_inner, grad_step, grad_output, grad_inner_taps, grad_head, grad_gated_gain), "dp"
    )
    shared = lax.psum((grad_state, grad_input_gain, grad_state_taps), ("dp", "tensor"))
    dp_place = lax.axis_index("dp")
    all_place = lax.axis_index(("dp", "tensor"))
    shard = inner_weight.shape[1]
    grad_inner = lax.dynamic_slice_in_dim(summed[0], dp_place * shard, shard, 1)
    grad_step = lax.dynamic_slice_in_dim(summed[1], dp_place * shard, shard, 0)
    grad_output = lax.dynamic_slice_in_dim(summed[2], dp_place * shard, shard, 1)
    grad_inner_taps = summed[3]
    grad_head = summed[4]
    grad_gated_gain = summed[5]
    state_rows = state_weight.shape[0]
    grad_state = lax.dynamic_slice_in_dim(shared[0], all_place * state_rows, state_rows, 0)
    grad_input_gain = shared[1]
    grad_state_taps = shared[2]
    grads = (
        grad_input_gain,
        grad_inner,
        grad_step,
        grad_state,
        grad_inner_taps,
        grad_state_taps,
        grad_head,
        grad_gated_gain,
        grad_output,
    )
    stepped = [
        adam_step(param, first, second_moment, grad, rate)
        for param, first, second_moment, grad, rate in zip(params, firsts, seconds, grads, rates)
    ]
    moved = [entry[0] for entry in stepped]
    first_new = [entry[1] for entry in stepped]
    second_new = [entry[2] for entry in stepped]
    return (result, gradient_hidden, *grads, *moved, *first_new, *second_new)


def solution(mesh):
    placed = (
        P("tensor", "dp", None),
        P("tensor", "dp", None),
        P(),
        P(None, "dp", "tensor"),
        P("dp", "tensor"),
        P(("dp", "tensor"), None),
        P(None, "tensor"),
        P(),
        P(None, "tensor"),
        P("tensor"),
        P("tensor", "dp"),
        P(),
        P(None, "dp", "tensor"),
        P("dp", "tensor"),
        P(("dp", "tensor"), None),
        P(None, "tensor"),
        P(),
        P(None, "tensor"),
        P("tensor"),
        P("tensor", "dp"),
        P(),
        P(None, "dp", "tensor"),
        P("dp", "tensor"),
        P(("dp", "tensor"), None),
        P(None, "tensor"),
        P(),
        P(None, "tensor"),
        P("tensor"),
        P("tensor", "dp"),
    )
    return jax.shard_map(
        body,
        mesh=mesh,
        in_specs=placed,
        out_specs=(
            P("tensor", "dp", None),
            P("tensor", "dp", None),
            P(),
            P(None, "dp", "tensor"),
            P("dp", "tensor"),
            P(("dp", "tensor"), None),
            P(None, "tensor"),
            P(),
            P(None, "tensor"),
            P("tensor"),
            P("tensor", "dp"),
            P(),
            P(None, "dp", "tensor"),
            P("dp", "tensor"),
            P(("dp", "tensor"), None),
            P(None, "tensor"),
            P(),
            P(None, "tensor"),
            P("tensor"),
            P("tensor", "dp"),
            P(),
            P(None, "dp", "tensor"),
            P("dp", "tensor"),
            P(("dp", "tensor"), None),
            P(None, "tensor"),
            P(),
            P(None, "tensor"),
            P("tensor"),
            P("tensor", "dp"),
            P(),
            P(None, "dp", "tensor"),
            P("dp", "tensor"),
            P(("dp", "tensor"), None),
            P(None, "tensor"),
            P(),
            P(None, "tensor"),
            P("tensor"),
            P("tensor", "dp"),
        ),
        check_vma=False,
    )
```

profile of v0, /device:TPU:0, one launch (start us, length us, event | category | flops | bytes accessed | tf_op | source)
XLA Modules:
  0.0 1778.5 jit_solution(4367595454640015792)
XLA Ops:
  31.0 74.1 %all_gather.21 = bf16[1536,256]{1,0:T(8,128)(2,1)S(1)} all-gather(bf16[48,256]{1,0:T(8,128)(2,1)S(1)} %convert_element_type.59), channel_id=1, replica_groups=mesh['dp'=8,'tensor'=4] {'dp','tensor'}, dimensions={0}, use_global_device_ids=true | all-gather | bytes 811008 | tf_op jit(solution)/shard_map/all_gather | solution.py:181
  118.5 33.3 %all-gather.8.cloned.1.call-done = bf16[2,1536,768]{2,1,0:T(8,128)(2,1)} async-done(((bf16[2,192,768]{2,1,0:T(8,128)(2,1)}), bf16[2,1536,768]{2,1,0:T(8,128)(2,1)}) %all-gather.8.cloned.1.call-update) | async-done | bytes 4718608 | tf_op jit(solution)/shard_map/all_gather | solution.py:177
  187.3 253.9 %while.44 = (s32[]{:T(128)}, f32[1,12,128,64]{2,3,1,0:T(8,128)S(1)}, f32[8,256,1,12,64]{1,0,4,3,2:T(8,128)}, f32[8,1,12,128,64]{3,4,2,1,0:T(8,128)}, f32[8,256,1...) while((s32[]{:T(128)}, ...), condition=%wide.region_4.5_spmd.clone.clone, body=%wide.region_1.4_spmd.clone.clone.sunk | while | flops 1313839104 | bytes 11464031 | solution.py:71
  201.1 18.5 %dynamic_update_slice.87 = f32[8,256,1,12,64]{1,0,4,3,2:T(8,128)} dynamic-update-slice(f32[8,256,1,12,64]{1,0,4,3,2:T(8,128)} %get-tuple-element.1404, f32[1,256,1,12,64]{1,0,4,3,2:T(1,128)S(1)} %copy.481, s32[]{:T(128)S(6)} %copy.493, s32[]{:T(128)} %constant.223.clone.1..sunk.1, s32[]{:T(128)} %constant.223.clone.1..sunk.1, s32[]{:T(128)} %constant.223.clone.1..sunk.1, s32[]{:T(128)} %constant.223.clone.1..sunk.1) | dynamic-update-slice | bytes 1572868 | tf_op jit(solution)/shard_map/jvp()/while/body/jit(dynamic_update_index_in_dim)/dynamic_update_slice | solution.py:71
  232.8 18.5 %dynamic_update_slice.87 = f32[8,256,1,12,64]{1,0,4,3,2:T(8,128)} dynamic-update-slice(f32[8,256,1,12,64]{1,0,4,3,2:T(8,128)} %get-tuple-element.1404, f32[1,256,1,12,64]{1,0,4,3,2:T(1,128)S(1)} %copy.481, s32[]{:T(128)S(6)} %copy.493, s32[]{:T(128)} %constant.223.clone.1..sunk.1, s32[]{:T(128)} %constant.223.clone.1..sunk.1, s32[]{:T(128)} %constant.223.clone.1..sunk.1, s32[]{:T(128)} %constant.223.clone.1..sunk.1) | dynamic-update-slice | bytes 1572868 | tf_op jit(solution)/shard_map/jvp()/while/body/jit(dynamic_update_index_in_dim)/dynamic_update_slice | solution.py:71
  264.4 18.5 %dynamic_update_slice.87 = f32[8,256,1,12,64]{1,0,4,3,2:T(8,128)} dynamic-update-slice(f32[8,256,1,12,64]{1,0,4,3,2:T(8,128)} %get-tuple-element.1404, f32[1,256,1,12,64]{1,0,4,3,2:T(1,128)S(1)} %copy.481, s32[]{:T(128)S(6)} %copy.493, s32[]{:T(128)} %constant.223.clone.1..sunk.1, s32[]{:T(128)} %constant.223.clone.1..sunk.1, s32[]{:T(128)} %constant.223.clone.1..sunk.1, s32[]{:T(128)} %constant.223.clone.1..sunk.1) | dynamic-update-slice | bytes 1572868 | tf_op jit(solution)/shard_map/jvp()/while/body/jit(dynamic_update_index_in_dim)/dynamic_update_slice | solution.py:71
  296.1 18.5 %dynamic_update_slice.87 = f32[8,256,1,12,64]{1,0,4,3,2:T(8,128)} dynamic-update-slice(f32[8,256,1,12,64]{1,0,4,3,2:T(8,128)} %get-tuple-element.1404, f32[1,256,1,12,64]{1,0,4,3,2:T(1,128)S(1)} %copy.481, s32[]{:T(128)S(6)} %copy.493, s32[]{:T(128)} %constant.223.clone.1..sunk.1, s32[]{:T(128)} %constant.223.clone.1..sunk.1, s32[]{:T(128)} %constant.223.clone.1..sunk.1, s32[]{:T(128)} %constant.223.clone.1..sunk.1) | dynamic-update-slice | bytes 1572868 | tf_op jit(solution)/shard_map/jvp()/while/body/jit(dynamic_update_index_in_dim)/dynamic_update_slice | solution.py:71
  327.8 18.5 %dynamic_update_slice.87 = f32[8,256,1,12,64]{1,0,4,3,2:T(8,128)} dynamic-update-slice(f32[8,256,1,12,64]{1,0,4,3,2:T(8,128)} %get-tuple-element.1404, f32[1,256,1,12,64]{1,0,4,3,2:T(1,128)S(1)} %copy.481, s32[]{:T(128)S(6)} %copy.493, s32[]{:T(128)} %constant.223.clone.1..sunk.1, s32[]{:T(128)} %constant.223.clone.1..sunk.1, s32[]{:T(128)} %constant.223.clone.1..sunk.1, s32[]{:T(128)} %constant.223.clone.1..sunk.1) | dynamic-update-slice | bytes 1572868 | tf_op jit(solution)/shard_map/jvp()/while/body/jit(dynamic_update_index_in_dim)/dynamic_update_slice | solution.py:71
  359.4 18.5 %dynamic_update_slice.87 = f32[8,256,1,12,64]{1,0,4,3,2:T(8,128)} dynamic-update-slice(f32[8,256,1,12,64]{1,0,4,3,2:T(8,128)} %get-tuple-element.1404, f32[1,256,1,12,64]{1,0,4,3,2:T(1,128)S(1)} %copy.481, s32[]{:T(128)S(6)} %copy.493, s32[]{:T(128)} %constant.223.clone.1..sunk.1, s32[]{:T(128)} %constant.223.clone.1..sunk.1, s32[]{:T(128)} %constant.223.clone.1..sunk.1, s32[]{:T(128)} %constant.223.clone.1..sunk.1) | dynamic-update-slice | bytes 1572868 | tf_op jit(solution)/shard_map/jvp()/while/body/jit(dynamic_update_index_in_dim)/dynamic_update_slice | solution.py:71
  391.1 18.5 %dynamic_update_slice.87 = f32[8,256,1,12,64]{1,0,4,3,2:T(8,128)} dynamic-update-slice(f32[8,256,1,12,64]{1,0,4,3,2:T(8,128)} %get-tuple-element.1404, f32[1,256,1,12,64]{1,0,4,3,2:T(1,128)S(1)} %copy.481, s32[]{:T(128)S(6)} %copy.493, s32[]{:T(128)} %constant.223.clone.1..sunk.1, s32[]{:T(128)} %constant.223.clone.1..sunk.1, s32[]{:T(128)} %constant.223.clone.1..sunk.1, s32[]{:T(128)} %constant.223.clone.1..sunk.1) | dynamic-update-slice | bytes 1572868 | tf_op jit(solution)/shard_map/jvp()/while/body/jit(dynamic_update_index_in_dim)/dynamic_update_slice | solution.py:71
  422.8 18.5 %dynamic_update_slice.87 = f32[8,256,1,12,64]{1,0,4,3,2:T(8,128)} dynamic-update-slice(f32[8,256,1,12,64]{1,0,4,3,2:T(8,128)} %get-tuple-element.1404, f32[1,256,1,12,64]{1,0,4,3,2:T(1,128)S(1)} %copy.481, s32[]{:T(128)S(6)} %copy.493, s32[]{:T(128)} %constant.223.clone.1..sunk.1, s32[]{:T(128)} %constant.223.clone.1..sunk.1, s32[]{:T(128)} %constant.223.clone.1..sunk.1, s32[]{:T(128)} %constant.223.clone.1..sunk.1) | dynamic-update-slice | bytes 1572868 | tf_op jit(solution)/shard_map/jvp()/while/body/jit(dynamic_update_index_in_dim)/dynamic_update_slice | solution.py:71
  548.6 462.0 %while.43 = (s32[]{:T(128)}, f32[1,12,128,64]{2,3,1,0:T(8,128)S(1)}, f32[8,256,1,12,64]{1,0,4,3,2:T(8,128)}, f32[8,256,1,12]{3,1,2,0:T(8,128)}, f32[8,256,1,12]{...) while((s32[]{:T(128)}, ...), condition=%wide.region_23.24_spmd.clone, body=%wide.region_10.23_spmd.clone.sunk | while | flops 3038768128 | bytes 32287520 | solution.py:71
  588.2 18.5 %dynamic_update_slice.84 = f32[8,256,1,12,64]{1,0,4,3,2:T(8,128)} dynamic-update-slice(f32[8,256,1,12,64]{1,0,4,3,2:T(8,128)} %get-tuple-element.1448, f32[1,256,1,12,64]{1,0,4,3,2:T(1,128)S(1)} %copy.466, s32[]{:T(128)S(6)} %sub.383, s32[]{:T(128)} %constant.223.clone.1..sunk, s32[]{:T(128)} %constant.223.clone.1..sunk, s32[]{:T(128)} %constant.223.clone.1..sunk, s32[]{:T(128)} %constant.223.clone.1..sunk) | dynamic-update-slice | bytes 1572868 | tf_op jit(solution)/shard_map/transpose(jvp())/while/body/jit(dynamic_update_index_in_dim)/dynamic_update_slice | solution.py:71
  645.9 18.5 %dynamic_update_slice.84 = f32[8,256,1,12,64]{1,0,4,3,2:T(8,128)} dynamic-update-slice(f32[8,256,1,12,64]{1,0,4,3,2:T(8,128)} %get-tuple-element.1448, f32[1,256,1,12,64]{1,0,4,3,2:T(1,128)S(1)} %copy.466, s32[]{:T(128)S(6)} %sub.383, s32[]{:T(128)} %constant.223.clone.1..sunk, s32[]{:T(128)} %constant.223.clone.1..sunk, s32[]{:T(128)} %constant.223.clone.1..sunk, s32[]{:T(128)} %constant.223.clone.1..sunk) | dynamic-update-slice | bytes 1572868 | tf_op jit(solution)/shard_map/transpose(jvp())/while/body/jit(dynamic_update_index_in_dim)/dynamic_update_slice | solution.py:71
  761.2 18.5 %dynamic_update_slice.84 = f32[8,256,1,12,64]{1,0,4,3,2:T(8,128)} dynamic-update-slice(f32[8,256,1,12,64]{1,0,4,3,2:T(8,128)} %get-tuple-element.1448, f32[1,256,1,12,64]{1,0,4,3,2:T(1,128)S(1)} %copy.466, s32[]{:T(128)S(6)} %sub.383, s32[]{:T(128)} %constant.223.clone.1..sunk, s32[]{:T(128)} %constant.223.clone.1..sunk, s32[]{:T(128)} %constant.223.clone.1..sunk, s32[]{:T(128)} %constant.223.clone.1..sunk) | dynamic-update-slice | bytes 1572868 | tf_op jit(solution)/shard_map/transpose(jvp())/while/body/jit(dynamic_update_index_in_dim)/dynamic_update_slice | solution.py:71
  876.6 18.5 %dynamic_update_slice.84 = f32[8,256,1,12,64]{1,0,4,3,2:T(8,128)} dynamic-update-slice(f32[8,256,1,12,64]{1,0,4,3,2:T(8,128)} %get-tuple-element.1448, f32[1,256,1,12,64]{1,0,4,3,2:T(1,128)S(1)} %copy.466, s32[]{:T(128)S(6)} %sub.383, s32[]{:T(128)} %constant.223.clone.1..sunk, s32[]{:T(128)} %constant.223.clone.1..sunk, s32[]{:T(128)} %constant.223.clone.1..sunk, s32[]{:T(128)} %constant.223.clone.1..sunk) | dynamic-update-slice | bytes 1572868 | tf_op jit(solution)/shard_map/transpose(jvp())/while/body/jit(dynamic_update_index_in_dim)/dynamic_update_slice | solution.py:71
  934.3 18.5 %dynamic_update_slice.84 = f32[8,256,1,12,64]{1,0,4,3,2:T(8,128)} dynamic-update-slice(f32[8,256,1,12,64]{1,0,4,3,2:T(8,128)} %get-tuple-element.1448, f32[1,256,1,12,64]{1,0,4,3,2:T(1,128)S(1)} %copy.466, s32[]{:T(128)S(6)} %sub.383, s32[]{:T(128)} %constant.223.clone.1..sunk, s32[]{:T(128)} %constant.223.clone.1..sunk, s32[]{:T(128)} %constant.223.clone.1..sunk, s32[]{:T(128)} %constant.223.clone.1..sunk) | dynamic-update-slice | bytes 1572868 | tf_op jit(solution)/shard_map/transpose(jvp())/while/body/jit(dynamic_update_index_in_dim)/dynamic_update_slice | solution.py:71
  992.0 18.5 %dynamic_update_slice.84 = f32[8,256,1,12,64]{1,0,4,3,2:T(8,128)} dynamic-update-slice(f32[8,256,1,12,64]{1,0,4,3,2:T(8,128)} %get-tuple-element.1448, f32[1,256,1,12,64]{1,0,4,3,2:T(1,128)S(1)} %copy.466, s32[]{:T(128)S(6)} %sub.383, s32[]{:T(128)} %constant.223.clone.1..sunk, s32[]{:T(128)} %constant.223.clone.1..sunk, s32[]{:T(128)} %constant.223.clone.1..sunk, s32[]{:T(128)} %constant.223.clone.1..sunk) | dynamic-update-slice | bytes 1572868 | tf_op jit(solution)/shard_map/transpose(jvp())/while/body/jit(dynamic_update_index_in_dim)/dynamic_update_slice | solution.py:71
  1028.3 19.1 %multiply_reduce_fusion.7 = (f32[768]{0:T(1024)S(1)}, f32[768]{0:T(1024)S(1)}, f32[768]{0:T(1024)S(1)}, f32[768]{0:T(1024)S(1)}, f32[768]{0:T(1024)S(1)}, /*index=5*/f32[2048,1,768]{2,0,1:T(8,128)}) fusion(f32[2048,768]{1,0:T(8,128)} %copy-done, f32[2048,1,768]{2,0,1:T(8,128)} %bitcast.640, f32[2048,1,768]{2,0,1:T(8,128)} %get-tuple-element.1139, ...), kind=kLoop, calls=%fused_computation.193 | loop fusion | flops 31453440 | bytes 37767168 | tf_op jit(solution)/shard_map/transpose(jvp())/reduce_sum | solution.py:38
  1149.6 26.4 %all-reduce.27 = (f32[5,768]{1,0:T(8,128)S(1)}, f32[3,12]{1,0:T(4,128)S(1)}, f32[768]{0:T(1024)S(1)}) all-reduce(f32[5,768]{1,0:T(8,128)S(1)} %pad_add_fusion.6, f32[3,12]{1,0:T(4,128)S(1)} %pad_add_fusion.8, f32[768]{0:T(1024)S(1)} %copy-done.92), channel_id=1, replica_groups=mesh['dp'=8,'tensor'=4] {'dp'}, use_global_device_ids=true, to_apply=%region_36.37 | all-reduce | flops 4644 | bytes 37152 | tf_op jit(solution)/shard_map/psum | solution.py:259
  1186.2 287.0 %all-reduce.34.cloned.1.call-done = (f32[2,1536,768]{2,1,0:T(8,128)}, f32[1536,12]{0,1:T(8,128)}, f32[768,1536]{0,1:T(8,128)}) async-done(((f32[2,1536,768]{2,1,0:T(8,128)}, f32[1536,12]{0,1:T(8,128)}, f32[768,1536]{0,1:T(8,128)}), (f32[2,1536,768]{2,1,0:T(8,128)}, f32[1536,12]{0,1:T(8,128)}, f32[768,1536]{0,1:T(8,128)})) %all-reduce.34.cloned.1.call-update) | async-done | bytes 14229520 | tf_op jit(solution)/shard_map/psum | solution.py:259
  1481.9 115.1 %reduce-scatter.5.cloned.1.call-done = f32[512,1536]{1,0:T(8,128)} async-done(((f32[2048,1536]{1,0:T(8,128)}), f32[512,1536]{1,0:T(8,128)}) %reduce-scatter.5.cloned.1.call-update) | async-done | bytes 3145744 | tf_op jit(solution)/shard_map/reduce_scatter | solution.py:245
  1599.7 121.0 %reduce-scatter.3.cloned.1.call-done = f32[512,1536]{1,0:T(8,128)} async-done(((f32[2048,1536]{1,0:T(8,128)}), f32[512,1536]{1,0:T(8,128)}) %reduce-scatter.3.cloned.1.call-update) | async-done | bytes 3145744 | tf_op jit(solution)/shard_map/reduce_scatter | solution.py:205
  1730.7 39.4 %all-reduce.26 = (f32[1536]{0:T(1024)S(1)}, f32[5,256]{1,0:T(8,128)S(1)}) all-reduce(f32[1536]{0:T(1024)S(1)} %get-tuple-element.1016, f32[5,256]{1,0:T(8,128)S(1)} %pad_add_fusion.7), channel_id=1, replica_groups=mesh['dp'=8,'tensor'=4] {'dp','tensor'}, use_global_device_ids=true, to_apply=%region_27.28 | all-reduce | flops 2816 | bytes 22528 | tf_op jit(solution)/shard_map/psum | solution.py:262
  (1152 shorter events, 784.7 us)
Async XLA Ops:
  7.2 97.9 %all-gather.6.cloned.1.call-start = ((), (), s32[]{:S(2)}) async-start(), calls=%async_computation.2 | async-start | bytes 7864320 | tf_op jit(solution)/shard_map/all_gather | solution.py:173
  12.3 139.5 %all-gather.8.cloned.1.call-start = ((), (), s32[]{:S(2)}) async-start(), calls=%async_computation.3 | async-start | bytes 5308416 | tf_op jit(solution)/shard_map/all_gather | solution.py:177
  13.3 468.2 %all-gather.10.cloned.1.call-start = ((), (), s32[]{:S(2)}) async-start(), calls=%async_computation.4 | async-start | bytes 2654208 | tf_op jit(solution)/shard_map/all_gather | solution.py:179
  14.1 467.4 %all-gather.12.cloned.1.call-start = ((), (), s32[]{:S(2)}) async-start(), calls=%async_computation.6 | async-start | bytes 7864320 | tf_op jit(solution)/shard_map/all_gather | solution.py:174
  14.7 1170.0 %all-reduce.32.cloned.1.call-start = ((), (), s32[]{:S(2)}) async-start(), calls=%async_computation.8 | async-start | bytes 3145728 | tf_op jit(solution)/shard_map/psum | solution.py:262
  15.0 486.0 %copy-start.60 = (f32[768]{0:T(1024)}, f32[768]{0:T(1024)S(1)}, u32[]{:S(2)}) copy-start(f32[768]{0:T(1024)S(1)} %mul.1116) | copy-start | bytes 9220
  15.1 144.8 %copy-start.52 = (f32[768]{0:T(1024)}, f32[768]{0:T(1024)S(1)}, u32[]{:S(2)}) copy-start(f32[768]{0:T(1024)S(1)} %get-tuple-element.1027) | copy-start | bytes 9220
  15.1 144.8 %copy-start.54 = (f32[768]{0:T(1024)}, f32[768]{0:T(1024)S(1)}, u32[]{:S(2)}) copy-start(f32[768]{0:T(1024)S(1)} %get-tuple-element.1028) | copy-start | bytes 9220
  15.1 144.8 %copy-start.56 = (f32[768]{0:T(1024)}, f32[768]{0:T(1024)S(1)}, u32[]{:S(2)}) copy-start(f32[768]{0:T(1024)S(1)} %get-tuple-element.1029) | copy-start | bytes 9220
  15.2 144.8 %copy-start.58 = (f32[768]{0:T(1024)}, f32[768]{0:T(1024)S(1)}, u32[]{:S(2)}) copy-start(f32[768]{0:T(1024)S(1)} %get-tuple-element.1030) | copy-start | bytes 9220
  1054.1 419.1 %all-reduce.34.cloned.1.call-start = ((), (), s32[]{:S(2)}) async-start(), calls=%async_computation.9 | async-start | bytes 28508160 | tf_op jit(solution)/shard_map/psum | solution.py:259
  1093.8 503.1 %reduce-scatter.5.cloned.1.call-start = ((), (), s32[]{:S(2)}) async-start(), calls=%async_computation.7 | async-start | bytes 15728640 | tf_op jit(solution)/shard_map/reduce_scatter | solution.py:245
  1137.2 583.5 %reduce-scatter.3.cloned.1.call-start = ((), (), s32[]{:S(2)}) async-start(), calls=%async_computation.5 | async-start | bytes 15728640 | tf_op jit(solution)/shard_map/reduce_scatter | solution.py:205
  1148.8 324.4 %copy-start.45 = (f32[192,12]{0,1:T(8,128)S(1)}, f32[192,12]{0,1:T(8,128)}, u32[]{:S(2)}) copy-start(f32[192,12]{0,1:T(8,128)} %param.37) | copy-start | bytes 27652
  1148.8 324.4 %copy-start.70 = (f32[192,12]{0,1:T(8,128)S(1)}, f32[192,12]{0,1:T(8,128)}, u32[]{:S(2)}) copy-start(f32[192,12]{0,1:T(8,128)} %param.46) | copy-start | bytes 27652
  1148.8 324.4 %copy-start.71 = (f32[192,12]{0,1:T(8,128)S(1)}, f32[192,12]{0,1:T(8,128)}, u32[]{:S(2)}) copy-start(f32[192,12]{0,1:T(8,128)} %param.55) | copy-start | bytes 27652
  1148.8 325.8 %copy-start.23 = (f32[768,192]{0,1:T(8,128)S(1)}, f32[768,192]{0,1:T(8,128)}, u32[]{:S(2)}) copy-start(f32[768,192]{0,1:T(8,128)} %param.43) | copy-start | bytes 1769476
  1148.8 325.8 %copy-start.27 = (f32[768,192]{0,1:T(8,128)S(1)}, f32[768,192]{0,1:T(8,128)}, u32[]{:S(2)}) copy-start(f32[768,192]{0,1:T(8,128)} %param.52) | copy-start | bytes 1769476
  1148.9 325.8 %copy-start.28 = (f32[768,192]{0,1:T(8,128)S(1)}, f32[768,192]{0,1:T(8,128)}, u32[]{:S(2)}) copy-start(f32[768,192]{0,1:T(8,128)} %param.61) | copy-start | bytes 1769476
  1148.9 328.3 %copy-start.13 = (f32[2,192,768]{2,1,0:T(8,128)S(1)}, f32[2,192,768]{2,1,0:T(8,128)}, u32[]{:S(2)}) copy-start(f32[2,192,768]{2,1,0:T(8,128)} %param.36) | copy-start | bytes 3538948
  1176.1 305.8 %copy-start.66 = (f32[5,768]{1,0:T(8,128)}, f32[5,768]{1,0:T(8,128)S(1)}, u32[]{:S(2)}) copy-start(f32[5,768]{1,0:T(8,128)S(1)} %get-tuple-element.1081) | copy-start | bytes 46084
  1176.1 305.8 %copy-start.93 = (f32[768]{0:T(1024)}, f32[768]{0:T(1024)S(1)}, u32[]{:S(2)}) copy-start(f32[768]{0:T(1024)S(1)} %get-tuple-element.1083) | copy-start | bytes 9220
  1176.1 305.8 %copy-start.96 = (f32[3,12]{1,0:T(4,128)}, f32[3,12]{1,0:T(4,128)S(1)}, u32[]{:S(2)}) copy-start(f32[3,12]{1,0:T(4,128)S(1)} %get-tuple-element.1082) | copy-start | bytes 436
  1481.8 238.8 %copy-start.11 = (bf16[512,1,1536]{2,0,1:T(8,128)(2,1)S(1)}, bf16[512,1,1536]{2,0,1:T(8,128)(2,1)}, u32[]{:S(2)}) copy-start(bf16[512,1,1536]{2,0,1:T(8,128)(2,1)} %param.34) | copy-start | bytes 4718596
  (171 other events, 3005.6 us)
Sparse Core Ops, SparseCore 0:
  12.4 85.9 all-gather.5
  100.6 51.1 all-gather.7
  154.0 30.1 all-gather.9
  186.0 69.2 all-gather.11
  1054.2 130.4 all-reduce.31
  1187.7 285.4 all-reduce.33
  1476.3 120.6 reduce-scatter.4
  1600.0 120.5 reduce-scatter.2
where the time goes:
time: 1790 us; the launch traced here: 1780 us
  waiting for transfers between devices  564 us (32%)
  local copies, waits for them, and re-layouts  509 us (28%)
  matrix products  351 us (20%)
  blocking collectives  174 us (10%)
  other arithmetic  161 us (9%)
    dynamic_update_slice x64, local copies, waits for them, and re-layouts, scan_heads(): lax.scan(jax.checkpoint(group_step), start, (split(inputs), split(steps),...  332 us
    psum x1, waiting for transfers between devices, body(): lax.psum((grad_inner, grad_step, grad_output, grad_inner_taps, grad_head,...  287 us
    reduce_scatter x1, waiting for transfers between devices, body(): lax.psum_scatter(jnp.dot(normed_out, output_b, preferred_element_type=jnp...  121 us
    dot_general x24, matrix products, group_step(): jnp.einsum('qksh,kshp->qshp', mixing, inputs, precision=precise_setting)  118 us
    reduce_scatter x1, waiting for transfers between devices, body(): lax.psum_scatter(piece(gate_flat, inner_b[0]) + piece(inner_flat, inner_b...  115 us
    all_gather x1, blocking collectives, body(): lax.all_gather(state_weight.astype(jnp.bfloat16), ('dp', 'tensor'), axis=...  74.1 us
    dot_general x5, matrix products, contract_last(): lax.dot_general(values, weight, (((1,), (1,)), ((), ())), preferred_eleme...  54 us
    unnamed x194, local copies, waits for them, and re-layouts  47.2 us
  transfers between devices with their start and end apart: 8, of which 5 were waited for; matrix products, arithmetic and copies ran while one was open for 25% of the time, Pallas kernels for 0%

commit v1 on v0

v1 whole, which is shorter than its diff:
```python
import functools
import jax
import jax.numpy as jnp
from jax import lax
from jax.experimental import pallas as pl
from jax.experimental.pallas import tpu as pltpu
from jax.sharding import PartitionSpec as P

GROUP = 256
norm_eps = 1e-05
beta_first = 0.9
beta_second = 0.95
adam_eps = 1e-08
decay_rate = 0.1
step_count = 4.0
rates = (0.2, 0.008, 0.008, 0.008, 0.1, 0.1, 0.4, 0.2, 0.006)

LANES = 128
CARRY = 8
BLOCKED = -1e30
f32 = jnp.float32
bf16 = jnp.bfloat16


def mm(a, b):
    return lax.dot_general(a, b, (((1,), (0,)), ((), ())), preferred_element_type=f32)


def mm_nt(a, b):
    return lax.dot_general(a, b, (((1,), (1,)), ((), ())), preferred_element_type=f32)


def mm_exact(a, b):
    return lax.dot_general(
        a, b, (((1,), (0,)), ((), ())), precision=lax.Precision.HIGHEST, preferred_element_type=f32
    )


def mm_split(values, weight):
    high = values.astype(bf16)
    low = (values - high.astype(f32)).astype(bf16)
    return mm(high, weight) + mm(low, weight)


def sigmoid(v):
    return 1.0 / (1.0 + jnp.exp(-v))


def tri_lower(count):
    rows = lax.broadcasted_iota(jnp.int32, (count, count), 0)
    cols = lax.broadcasted_iota(jnp.int32, (count, count), 1)
    return rows >= cols


def step_terms(step_pre, heads_ref):
    shifted = step_pre + heads_ref[1:2, :]
    steps = jnp.maximum(shifted, 0.0) + jnp.log1p(jnp.exp(-jnp.abs(shifted)))
    logs = heads_ref[0:1, :] * steps
    count = logs.shape[0]
    cumul = mm_exact(tri_lower(count).astype(f32), logs)
    return shifted, steps, logs, cumul


def forward_kernel(
    width, size, pre_ref, taps_ref, heads_ref, skip_ref, spread_ref,
    scanned_ref, conv_ref, gated_ref, squares_ref, states_ref,
    ext, state, act,
):
    count = pre_ref.shape[0]
    half = count // 2
    conv_width = taps_ref.shape[1]
    taps = taps_ref.shape[0] - 1
    state_size = (conv_width - width) // 2
    per_tile = LANES // size

    @pl.when(pl.program_id(1) == 0)
    def _():
        ext[0:CARRY, :] = jnp.zeros((CARRY, conv_width), f32)
        state[...] = jnp.zeros_like(state)

    states_ref[0] = state[...]
    for start in range(0, conv_width, LANES):
        cols = slice(start, start + LANES)
        ext[CARRY : CARRY + count, cols] = pre_ref[:, width + start : width + start + LANES]
        total = taps_ref[taps : taps + 1, cols]
        for j in range(taps):
            total = total + taps_ref[j : j + 1, cols] * ext[CARRY + 1 - taps + j : CARRY + 1 - taps + j + count, cols]
        conv_ref[:, cols] = total
        act[:, cols] = total * sigmoid(total)
        ext[0:CARRY, cols] = ext[count : count + CARRY, cols]

    shifted, steps, logs, cumul = step_terms(pre_ref[:, width + conv_width :], heads_ref)
    cumul_t = cumul.T
    final = cumul[count - 1 : count, :]
    decay_in = jnp.exp(cumul)
    decay_out = jnp.exp(final - cumul)
    keys = act[:, width : width + state_size].astype(bf16)
    queries = act[:, width + state_size :].astype(bf16)
    keys_t = act[:, width : width + state_size].T.astype(bf16)
    scores = mm_nt(queries, keys)
    causal = tri_lower(half)
    lane = lax.broadcasted_iota(jnp.int32, (count, LANES), 1)
    squares = jnp.zeros((count, LANES), f32)
    for tile in range(width // LANES):
        cols = slice(tile * LANES, (tile + 1) * LANES)
        spread = spread_ref[:, cols]
        inner = act[:, cols]
        scaled = inner * mm_split(steps, spread)
        scaled_b = scaled.astype(bf16)
        mixed = None
        for k in range(per_tile):
            head = tile * per_tile + k
            col = cumul[:, head : head + 1]
            row = cumul_t[head : head + 1, :]
            first = jnp.exp(jnp.where(causal, col[:half] - row[:, :half], BLOCKED)) * scores[:half, :half]
            low = jnp.exp(col[half:] - row[:, :half]) * scores[half:, :half]
            last = jnp.exp(jnp.where(causal, col[half:] - row[:, half:], BLOCKED)) * scores[half:, half:]
            top = mm(first.astype(bf16), scaled_b[:half])
            bottom = mm(jnp.concatenate([low.astype(bf16), last.astype(bf16)], axis=1), scaled_b)
            part = jnp.concatenate([top, bottom], axis=0)
            mixed = part if mixed is None else jnp.where(lane >= k * size, part, mixed)
        in_wide = mm_split(decay_in, spread)
        out_wide = mm_split(decay_out, spread)
        held = state[:, cols]
        scanned = mixed + in_wide * mm(queries, held.astype(bf16))
        state[:, cols] = in_wide[count - 1 : count, :] * held + mm(keys_t, (out_wide * scaled).astype(bf16))
        scanned_ref[:, cols] = scanned
        gate = pre_ref[:, cols]
        gated = (scanned + skip_ref[:, cols] * inner) * (gate * sigmoid(gate))
        gated_ref[:, cols] = gated
        squares = squares + gated * gated
    squares_ref[...] = jnp.sum(squares, axis=1, keepdims=True)


def backward_kernel(
    width, size, pre_ref, conv_ref, scanned_ref, dnormed_ref, token_ref, states_ref,
    taps_ref, heads_ref, skip_ref, gain_ref, spread_ref, gather_ref,
    dpre_ref, taps_grad_ref, wide_grad_ref, heads_grad_ref,
    ext, dstate, dscores, in_rows, out_rows, dstate_b, finals,
):
    count = pre_ref.shape[0]
    half = count // 2
    conv_width = taps_ref.shape[1]
    taps = taps_ref.shape[0] - 1
    state_size = (conv_width - width) // 2
    per_tile = LANES // size

    @pl.when(pl.program_id(1) == 0)
    def _():
        ext[count : count + CARRY, :] = jnp.zeros((CARRY, conv_width), f32)
        dstate[...] = jnp.zeros_like(dstate)

    @pl.when((pl.program_id(0) == 0) & (pl.program_id(1) == 0))
    def _():
        taps_grad_ref[...] = jnp.zeros_like(taps_grad_ref)
        wide_grad_ref[...] = jnp.zeros_like(wide_grad_ref)
        heads_grad_ref[...] = jnp.zeros_like(heads_grad_ref)

    shifted, steps, logs, cumul = step_terms(pre_ref[:, width + conv_width :], heads_ref)
    cumul_t = cumul.T
    final = cumul[count - 1 : count, :]
    decay_in = jnp.exp(cumul)
    decay_out = jnp.exp(final - cumul)
    key_cols = slice(width, width + state_size)
    query_cols = slice(width + state_size, conv_width)
    key_pre = conv_ref[:, key_cols]
    query_pre = conv_ref[:, query_cols]
    key_sig = sigmoid(key_pre)
    query_sig = sigmoid(query_pre)
    keys = (key_pre * key_sig).astype(bf16)
    queries = (query_pre * query_sig).astype(bf16)
    queries_t = (query_pre * query_sig).T.astype(bf16)
    scores_t = mm_nt(keys, queries)
    rows = lax.broadcasted_iota(jnp.int32, (half, half), 0)
    columns = lax.broadcasted_iota(jnp.int32, (half, half), 1)
    causal_t = columns >= rows
    lane = lax.broadcasted_iota(jnp.int32, (count, LANES), 1)
    dscores[...] = jnp.zeros_like(dscores)
    scale = token_ref[:, 0:1]
    pull = token_ref[:, 1:2]
    dcumul = jnp.zeros((count, LANES), f32)
    dsteps = jnp.zeros((count, LANES), f32)
    for tile in range(width // LANES):
        cols = slice(tile * LANES, (tile + 1) * LANES)
        spread = spread_ref[:, cols]
        gather = gather_ref[cols, :]
        conv = conv_ref[:, cols]
        sig = sigmoid(conv)
        inner = conv * sig
        gate = pre_ref[:, cols]
        gate_sig = sigmoid(gate)
        gate_act = gate * gate_sig
        scanned = scanned_ref[:, cols]
        mixed = scanned + skip_ref[:, cols] * inner
        gated = mixed * gate_act
        dnormed = dnormed_ref[:, cols]
        wide_grad_ref[0:1, cols] += jnp.sum(dnormed * gated * scale, axis=0, keepdims=True)
        dgated = scale * (dnormed * gain_ref[:, cols]) - pull * gated
        dmixed = dgated * gate_act
        dgate = dgated * mixed * (gate_sig * (1.0 + gate * (1.0 - gate_sig)))
        dpre_ref[:, cols] = dgate.astype(bf16)
        wide_grad_ref[1:2, cols] += jnp.sum(dmixed * inner, axis=0, keepdims=True)
        dmixed_b = dmixed.astype(bf16)
        steps_wide = mm_split(steps, spread)
        scaled = inner * steps_wide
        scaled_b = scaled.astype(bf16)
        dscaled = None
        for k in range(per_tile):
            head = tile * per_tile + k
            col = cumul[:, head : head + 1]
            row = cumul_t[head : head + 1, :]
            own = jnp.where((lane >= k * size) & (lane < (k + 1) * size), scaled, 0.0).astype(bf16)
            first = jnp.exp(jnp.where(causal_t, row[:, :half] - col[:half], BLOCKED))
            right = jnp.exp(row[:, half:] - col[:half])
            last = jnp.exp(jnp.where(causal_t, row[:, half:] - col[half:], BLOCKED))
            top = mm(
                jnp.concatenate(
                    [
                        (first * scores_t[:half, :half]).astype(bf16),
                        (right * scores_t[:half, half:]).astype(bf16),
                    ],
                    axis=1,
                ),
                dmixed_b,
            )
            bottom = mm((last * scores_t[half:, half:]).astype(bf16), dmixed_b[half:])
            part = jnp.concatenate([top, bottom], axis=0)
            dscaled = part if dscaled is None else jnp.where(lane >= k * size, part, dscaled)
            dscores[:half, :half] += mm_nt(own[:half], dmixed_b[:half]) * first
            dscores[:half, half:] += mm_nt(own[:half], dmixed_b[half:]) * right
            dscores[half:, half:] += mm_nt(own[half:], dmixed_b[half:]) * last
        in_wide = mm_split(decay_in, spread)
        out_wide = mm_split(decay_out, spread)
        dheld = dstate[:, cols]
        dheld_b = dheld.astype(bf16)
        dstate_b[:, cols] = dheld_b
        dlate = out_wide * mm(keys, dheld_b)
        dscaled = dscaled + dlate
        rounded = scaled_b.astype(f32)
        dcumul = dcumul + mm_split(dmixed_b.astype(f32) * scanned - rounded * dscaled, gather)
        dsteps = dsteps + mm_split(inner * dscaled, gather)
        final_wide = in_wide[count - 1 : count, :]
        finals[0:1, cols] = jnp.sum(rounded * dlate, axis=0, keepdims=True) + final_wide * jnp.sum(
            dheld * states_ref[0, :, cols], axis=0, keepdims=True
        )
        dinner = dscaled * steps_wide + skip_ref[:, cols] * dmixed
        ext[0:count, cols] = dinner * (sig * (1.0 + conv * (1.0 - sig)))
        in_b = (in_wide * dmixed).astype(bf16)
        in_rows[:, cols] = in_b
        out_rows[:, cols] = (out_wide * scaled).astype(bf16)
        dstate[:, cols] = final_wide * dheld + mm(queries_t, in_b)

    pairs = dscores[...]
    dkeys = mm(pairs.astype(bf16), queries) + mm_nt(out_rows[...], dstate_b[...])
    dqueries = mm(pairs.T.astype(bf16), keys) + mm_nt(in_rows[...], states_ref[0].astype(bf16))
    ext[0:count, key_cols] = dkeys * (key_sig * (1.0 + key_pre * (1.0 - key_sig)))
    ext[0:count, query_cols] = dqueries * (query_sig * (1.0 + query_pre * (1.0 - query_sig)))

    for start in range(0, conv_width, LANES):
        cols = slice(start, start + LANES)
        pre = pre_ref[:, width + start : width + start + LANES]
        total = None
        for j in range(taps):
            moved = ext[taps - 1 - j : taps - 1 - j + count, cols]
            term = taps_ref[j : j + 1, cols] * moved
            total = term if total is None else total + term
            taps_grad_ref[j : j + 1, cols] += jnp.sum(pre * moved, axis=0, keepdims=True)
        taps_grad_ref[taps : taps + 1, cols] += jnp.sum(ext[0:count, cols], axis=0, keepdims=True)
        dpre_ref[:, width + start : width + start + LANES] = total.astype(bf16)
        ext[count : count + CARRY, cols] = ext[0:CARRY, cols]

    final_row = mm_split(jnp.broadcast_to(finals[0:1, :], (CARRY, width)), gather_ref[...])[0:1]
    suffix = 1.0 - tri_lower(count).astype(f32) + jnp.where(
        lax.broadcasted_iota(jnp.int32, (count, count), 0)
        == lax.broadcasted_iota(jnp.int32, (count, count), 1),
        1.0,
        0.0,
    )
    dlogs = mm_exact(suffix, dcumul) + final_row
    dshifted = (dsteps + dlogs * heads_ref[0:1, :]) * sigmoid(shifted)
    dpre_ref[:, width + conv_width :] = dshifted.astype(bf16)
    heads_grad_ref[0:1, :] += jnp.sum(dlogs * logs, axis=0, keepdims=True)
    heads_grad_ref[1:2, :] += jnp.sum(dshifted, axis=0, keepdims=True)


def whole(shape):
    return pl.BlockSpec(shape, lambda s, i: (0,) * len(shape))


def run_forward(pre, taps, heads, skip, spread, seqs, count, size):
    rows, cat = pre.shape
    width = skip.shape[1]
    conv_width = taps.shape[1]
    state_size = (conv_width - width) // 2
    blocks = rows // seqs // count

    def block(cols):
        return pl.BlockSpec((count, cols), lambda s, i: (s * blocks + i, 0))

    return pl.pallas_call(
        functools.partial(forward_kernel, width, size),
        grid=(seqs, blocks),
        in_specs=[block(cat), whole(taps.shape), whole(heads.shape), whole(skip.shape), whole(spread.shape)],
        out_specs=[
            block(width), block(conv_width), block(width), block(1),
            pl.BlockSpec((1, state_size, width), lambda s, i: (s * blocks + i, 0, 0)),
        ],
        out_shape=[
            jax.ShapeDtypeStruct((rows, width), f32),
            jax.ShapeDtypeStruct((rows, conv_width), f32),
            jax.ShapeDtypeStruct((rows, width), f32),
            jax.ShapeDtypeStruct((rows, 1), f32),
            jax.ShapeDtypeStruct((seqs * blocks, state_size, width), f32),
        ],
        scratch_shapes=[
            pltpu.VMEM((count + CARRY, conv_width), f32),
            pltpu.VMEM((state_size, width), f32),
            pltpu.VMEM((count, conv_width), f32),
        ],
        cost_estimate=pl.CostEstimate(
            flops=rows * width * count * 4, bytes_accessed=rows * (cat + 4 * width) * 4, transcendentals=rows * count * 12
        ),
        name="mixer_forward",
    )(pre, taps, heads, skip, spread)


def run_backward(pre, conv, scanned, dnormed, token, states, taps, heads, skip, gain, spread, gather, seqs, count, size):
    rows, cat = pre.shape
    width = skip.shape[1]
    conv_width = taps.shape[1]
    state_size = (conv_width - width) // 2
    blocks = rows // seqs // count

    def block(cols):
        return pl.BlockSpec((count, cols), lambda s, i: (s * blocks + blocks - 1 - i, 0))

    return pl.pallas_call(
        functools.partial(backward_kernel, width, size),
        grid=(seqs, blocks),
        in_specs=[
            block(cat), block(conv_width), block(width), block(width), block(2),
            pl.BlockSpec((1, state_size, width), lambda s, i: (s * blocks + blocks - 1 - i, 0, 0)),
            whole(taps.shape), whole(heads.shape), whole(skip.shape), whole(gain.shape),
            whole(spread.shape), whole(gather.shape),
        ],
        out_specs=[block(cat), whole((8, conv_width)), whole((8, width)), whole((8, LANES))],
        out_shape=[
            jax.ShapeDtypeStruct((rows, cat), bf16),
            jax.ShapeDtypeStruct((8, conv_width), f32),
            jax.ShapeDtypeStruct((8, width), f32),
            jax.ShapeDtypeStruct((8, LANES), f32),
        ],
        scratch_shapes=[
            pltpu.VMEM((count + CARRY, conv_width), f32),
            pltpu.VMEM((state_size, width), f32),
            pltpu.VMEM((count, count), f32),
            pltpu.VMEM((count, width), bf16),
            pltpu.VMEM((count, width), bf16),
            pltpu.VMEM((state_size, width), bf16),
            pltpu.VMEM((8, width), f32),
        ],
        cost_estimate=pl.CostEstimate(
            flops=rows * width * count * 8, bytes_accessed=rows * (2 * cat + 4 * width) * 4, transcendentals=rows * count * 12
        ),
        name="mixer_backward",
    )(pre, conv, scanned, dnormed, token, states, taps, heads, skip, gain, spread, gather)


def adam_step(param, first, second_moment, grad, rate):
    first_new = beta_first * first + (1.0 - beta_first) * grad
    second_new = beta_second * second_moment + (1.0 - beta_second) * grad * grad
    first_hat = first_new / (1.0 - beta_first**step_count)
    second_hat = second_new / (1.0 - beta_second**step_count)
    moved = param - rate * (first_hat / (jnp.sqrt(second_hat) + adam_eps) + decay_rate * param)
    return (moved, first_new, second_new)


def body(hidden, cotangent, *arrays):
    params, firsts, seconds = arrays[:9], arrays[9:18], arrays[18:27]
    (
        input_gain,
        inner_weight,
        step_weight,
        state_weight,
        inner_taps,
        state_taps,
        head_params,
        gated_gain,
        output_matrix,
    ) = params
    local_len, seqs, features = hidden.shape
    wide = inner_taps.shape[1]
    heads = head_params.shape[1]
    size = wide // heads
    states = state_taps.shape[1]
    shards = lax.axis_size("tensor")
    length = local_len * shards
    rows = length * seqs
    inner_total = wide * shards

    base = hidden.astype(f32)
    rstd = lax.rsqrt(jnp.mean(base * base, -1, keepdims=True) + norm_eps)
    normed = base * rstd
    normed_in = (normed * input_gain).astype(bf16)

    def by_sequence(values):
        return values.transpose(1, 0, 2).reshape(values.shape[0] * seqs, values.shape[2])

    def by_position(values):
        return values.reshape(seqs, values.shape[0] // seqs, values.shape[1]).transpose(1, 0, 2)

    state_rows = lax.all_gather(state_weight.astype(bf16), "tensor", axis=0, tiled=True)
    full_in = lax.all_gather(normed_in, "tensor", axis=0, tiled=True)
    weights_own = jnp.concatenate(
        [
            inner_weight[0].astype(bf16),
            inner_weight[1].astype(bf16),
            state_rows,
            jnp.pad(step_weight.astype(bf16), ((0, 0), (0, LANES - heads))),
        ],
        axis=1,
    )
    weights = lax.all_gather(weights_own, "dp", axis=0, tiled=True)
    output_t = lax.all_gather(output_matrix.astype(bf16).T, "dp", axis=0, tiled=True)
    full_cot = lax.all_gather(cotangent, "tensor", axis=0, tiled=True)
    flat_in = by_sequence(full_in)
    flat_cot = by_sequence(full_cot)

    taps = jnp.concatenate([inner_taps, state_taps], axis=1)
    head_rows = jnp.pad(
        jnp.stack([-jnp.exp(head_params[0]), head_params[1]]), ((0, 0), (0, LANES - heads))
    )
    skip = jnp.repeat(head_params[2], size)[None]
    gain = gated_gain[None]
    spread = (jnp.arange(LANES)[:, None] == jnp.arange(wide)[None] // size).astype(bf16)
    gather = (jnp.arange(wide)[:, None] // size == jnp.arange(LANES)[None]).astype(bf16)

    pre = mm(flat_in, weights)
    scanned, conv, gated, squares, chunk_states = run_forward(
        pre, taps, head_rows, skip, spread, seqs, GROUP, size
    )
    d_normed = mm(flat_cot, output_t)
    crossed = jnp.sum(d_normed * gain * gated, -1, keepdims=True)
    sums = lax.psum(jnp.concatenate([squares, crossed], axis=1), "tensor")
    scale = lax.rsqrt(sums[:, 0:1] / inner_total + norm_eps)
    token = jnp.concatenate(
        [scale, scale * scale * scale * (sums[:, 1:2] / inner_total)], axis=1
    )
    normed_out = (gated * scale * gain).astype(bf16)
    branch = lax.psum_scatter(
        by_position(mm_nt(normed_out, output_t)).astype(bf16),
        "tensor",
        scatter_dimension=0,
        tiled=True,
    )
    result = (base + branch.astype(f32)).astype(bf16)
    grad_output_t = lax.psum_scatter(
        contract_first(flat_cot, normed_out).astype(bf16), "dp", scatter_dimension=0, tiled=True
    )

    d_pre, taps_grad, wide_grad, head_grad = run_backward(
        pre, conv, scanned, d_normed, token, chunk_states, taps, head_rows, skip, gain,
        spread, gather, seqs, GROUP, size,
    )
    d_in = lax.psum_scatter(
        by_position(mm_nt(d_pre, weights)).astype(bf16),
        "tensor",
        scatter_dimension=0,
        tiled=True,
    ).astype(f32)
    grad_weights = contract_first(flat_in, d_pre)
    grad_own = lax.psum_scatter(
        grad_weights.astype(bf16), "dp", scatter_dimension=0, tiled=True
    )
    grad_gain_rows = jnp.sum(grad_weights * weights.astype(f32), axis=1) / input_gain
    grad_state = lax.psum_scatter(
        grad_own[:, 2 * wide : 2 * wide + states].astype(f32),
        "tensor",
        scatter_dimension=0,
        tiled=True,
    )

    d_hat = d_in * input_gain
    gradient_hidden = cotangent.astype(f32) + rstd * (
        d_hat - normed * jnp.mean(d_hat * normed, -1, keepdims=True)
    )
    grad_skip = jnp.sum(wide_grad[1].reshape(heads, size), axis=1)
    split_terms = (
        taps_grad[: inner_taps.shape[0], :wide],
        jnp.concatenate([head_grad[:2, :heads], grad_skip[None]], axis=0),
        wide_grad[0],
    )
    shared_terms = (grad_gain_rows, taps_grad[: state_taps.shape[0], wide:])
    split_sums = lax.psum(split_terms, "dp")
    shared_sums = lax.psum(shared_terms, ("dp", "tensor"))
    own = grad_own.astype(f32)
    grads = (
        shared_sums[0],
        jnp.stack([own[:, :wide], own[:, wide : 2 * wide]]),
        own[:, 2 * wide + states : 2 * wide + states + heads],
        grad_state,
        split_sums[0],
        shared_sums[1],
        split_sums[1],
        split_sums[2],
        grad_output_t.astype(f32).T,
    )
    stepped = [
        adam_step(param, first, second_moment, grad, rate)
        for param, first, second_moment, grad, rate in zip(params, firsts, seconds, grads, rates)
    ]
    moved = [entry[0] for entry in stepped]
    first_new = [entry[1] for entry in stepped]
    second_new = [entry[2] for entry in stepped]
    return (result, gradient_hidden, *grads, *moved, *first_new, *second_new)


def contract_first(left, right):
    return lax.dot_general(left, right, (((0,), (0,)), ((), ())), preferred_element_type=f32)


def solution(mesh):
    weights = (
        P(),
        P(None, "dp", "tensor"),
        P("dp", "tensor"),
        P(("dp", "tensor"), None),
        P(None, "tensor"),
        P(),
        P(None, "tensor"),
        P("tensor"),
        P("tensor", "dp"),
    )
    rows = P("tensor", "dp", None)
    return jax.shard_map(
        body,
        mesh=mesh,
        in_specs=(rows, rows) + weights * 3,
        out_specs=(rows, rows) + weights * 4,
        check_vma=False,
    )
```

time: 1790 us -> 665 us (0.37)
  local copies, waits for them, and re-layouts: 509 us -> 45.2 us
  waiting for transfers between devices: 564 us -> 285 us
  matrix products: 351 us -> 89.6 us
  other arithmetic: 161 us -> 35.7 us
  Pallas kernels: 0 us -> 92.3 us
  blocking collectives: 174 us -> 93.8 us
    dynamic_update_slice x64 -> x0, local copies, waits for them, and re-layouts: 332 us -> none  [scan_heads(): lax.scan(jax.checkpoint(group_step), start, (split(inputs), split(steps),...]
    psum x2 -> x0, waiting for transfers between devices: 294 us -> none  [the longest x1 287 us: body(): lax.psum((grad_inner, grad_step, grad_output, grad_inner_taps, grad_head,...]
    dot_general x114 -> x4, matrix products: 310 us -> 58.9 us  [the longest x2 30 us: mm(): lax.dot_general(a, b, (((1,), (0,)), ((), ())), preferred_element_type=f32)]
    reduce_scatter x2 -> x3, waiting for transfers between devices: 236 us -> 59.2 us  [the longest x1 59.2 us: body(): lax.psum_scatter(by_position(mm_nt(normed_out, output_t)).astype(bf16), '...]
    all_gather x4, waiting for transfers between devices: 33.4 us -> 174 us  [the longest x1 63.7 us: body(): weights = lax.all_gather(weights_own, 'dp', axis=0, tiled=True)]
    pallas_call x0 -> x2, Pallas kernels: none -> 92.3 us  [the longest x1 63.1 us: run_backward(): pl.pallas_call(functools.partial(backward_kernel, width, size), grid=(seq...]
    all_gather x2 -> x1, blocking collectives: 89.8 us -> 9.97 us  [body(): lax.all_gather(state_weight.astype(bf16), 'tensor', axis=0, tiled=True)]
    unnamed x8 -> x11, waiting for transfers between devices: 0.64 us -> 51.8 us
  transfers between devices with their start and end apart: 8 -> 9, of which waited for: 5 -> 5; matrix products, arithmetic and copies ran while one was open for 25% -> 19% of each run, Pallas kernels for 0% -> 4%
where the time goes in v1:
time: 665 us; the launch traced here: 657 us
  waiting for transfers between devices  285 us (43%)
  blocking collectives  93.8 us (14%)
  Pallas kernels  92.3 us (14%)
  matrix products  89.6 us (13%)
  local copies, waits for them, and re-layouts  45.2 us (7%)
  other arithmetic  35.7 us (5%)
  between operations  14.6 us (2%)
    all_gather x1, waiting for transfers between devices, body(): weights = lax.all_gather(weights_own, 'dp', axis=0, tiled=True)  63.7 us
    pallas_call x1, Pallas kernels, run_backward(): pl.pallas_call(functools.partial(backward_kernel, width, size), grid=(seq...  63.1 us
    reduce_scatter x1, waiting for transfers between devices, body(): lax.psum_scatter(by_position(mm_nt(normed_out, output_t)).astype(bf16), '...  59.2 us
    all_gather x1, waiting for transfers between devices, body(): full_in = lax.all_gather(normed_in, 'tensor', axis=0, tiled=True)  56.6 us
    all_gather x1, waiting for transfers between devices, body(): full_cot = lax.all_gather(cotangent, 'tensor', axis=0, tiled=True)  53.4 us
    unnamed x11, waiting for transfers between devices  51.8 us
    psum x1, blocking collectives, body(): shared_sums = lax.psum(shared_terms, ('dp', 'tensor'))  38.7 us
    unnamed x62, local copies, waits for them, and re-layouts  34.2 us
  transfers between devices with their start and end apart: 9, of which 5 were waited for; matrix products, arithmetic and copies ran while one was open for 19% of the time, Pallas kernels for 4%

profile of v1, /device:TPU:0, one launch (start us, length us, event | category | flops | bytes accessed | tf_op | source)
XLA Modules:
  0.0 656.5 jit_solution(12556882222176932124)
XLA Ops:
  12.5 10.0 %all_gather.16 = bf16[192,256]{1,0:T(8,128)(2,1)S(1)} all-gather(bf16[48,256]{1,0:T(8,128)(2,1)S(1)} %convert_element_type.85), channel_id=1, replica_groups=mesh['dp'=8,'tensor'=4] {'tensor'}, dimensions={0}, use_global_device_ids=true | all-gather | bytes 122880 | tf_op jit(solution)/shard_map/all_gather | solution.py:412
  28.5 56.6 %all-gather.5.cloned.1.call-done = bf16[2048,1,1536]{2,0,1:T(8,128)(2,1)} async-done(((bf16[512,1,1536]{2,0,1:T(8,128)(2,1)}), bf16[2048,1,1536]{2,0,1:T(8,128)(2,1)}) %all-gather.5.cloned.1.call-update) | async-done | bytes 6291472 | tf_op jit(solution)/shard_map/all_gather | solution.py:413
  85.1 63.7 %all-gather.7.cloned.1.call-done = bf16[1536,1920]{1,0:T(8,128)(2,1)} async-done(((bf16[192,1920]{1,0:T(8,128)(2,1)}), bf16[1536,1920]{1,0:T(8,128)(2,1)}) %all-gather.7.cloned.1.call-update) | async-done | bytes 5898256 | tf_op jit(solution)/shard_map/all_gather | solution.py:423
  148.8 19.2 %fusion.8.pre_ref = f32[2048,1920]{1,0:T(8,128)} fusion(bf16[1536,1920]{1,0:T(8,128)(2,1)} %all-gather.7.cloned.1.call-done, bf16[2048,1,1536]{2,0,1:T(8,128)(2,1)} %all-gather.5.cloned.1.call-done), kind=kOutput, calls=%fused_computation.11 | convolution fusion | flops 12079595520 | bytes 27918336 | tf_op jit(solution)/shard_map/dot_general | solution.py:26
  168.0 29.2 %mixer_forward.1 = (f32[2048,768]{1,0:T(8,128)}, f32[2048,1024]{1,0:T(8,128)}, f32[2048,768]{1,0:T(8,128)}, f32[2048,1]{1,0:T(8,128)}, f32[8,128,768]{2,1,0:T(8,128)}) custom-call(f32[2048,1920]{1,0:T(8,128)} %fusion.8.pre_ref, f32[5,1024]{1,0:T(8,128)} %copy-done.9, f32[2,128]{1,0:T(2,128)} %select_maximum_fusion.heads_ref, ...), custom_call_target="tpu_custom_call" | custom-call | flops 1610612736 | bytes 40894464 | tf_op jit(solution)/shard_map/mixer_forward/pallas_call | solution.py:300
  198.7 53.4 %all-gather.9.cloned.1.call-done = bf16[2048,1,1536]{2,0,1:T(8,128)(2,1)} async-done(((bf16[512,1,1536]{2,0,1:T(8,128)(2,1)}), bf16[2048,1,1536]{2,0,1:T(8,128)(2,1)}) %all-gather.9.cloned.1.call-update) | async-done | bytes 6291472 | tf_op jit(solution)/shard_map/all_gather | solution.py:425
  252.2 10.7 %multiply_reduce_fusion.1 = (f32[2048]{0:T(1024)S(1)}, f32[2048,768]{1,0:T(8,128)}) fusion(f32[2048,768]{1,0:T(8,128)} %get-tuple-element.47, f32[768]{0:T(1024)S(1)} %copy-done.19, bf16[1536,768]{1,0:T(8,128)(2,1)} %all-gather.11.cloned.1.call-done, bf16[2048,1,1536]{2,0,1:T(8,128)(2,1)} %all-gather.9.cloned.1.call-done), kind=kOutput, calls=%fused_computation.14 | convolution fusion | flops 4836554752 | bytes 21244928 | tf_op jit(solution)/shard_map/dot_general | solution.py:26
  263.0 15.4 %psum.42 = f32[2048,2]{0,1:T(2,128)S(1)} all-reduce(f32[2048,2]{0,1:T(2,128)S(1)} %pad_maximum_fusion.1), channel_id=1, replica_groups=mesh['dp'=8,'tensor'=4] {'tensor'}, use_global_device_ids=true, to_apply=%region_2.3 | all-reduce | flops 4096 | bytes 32768 | tf_op jit(solution)/shard_map/psum | solution.py:444
  279.7 63.1 %mixer_backward.1 = (bf16[2048,1920]{1,0:T(8,128)(2,1)}, f32[8,1024]{1,0:T(8,128)}, f32[8,768]{1,0:T(8,128)}, f32[8,128]{1,0:T(8,128)}) custom-call(f32[2048,1920]{1,0:T(8,128)} %fusion.8.pre_ref, f32[2048,1024]{1,0:T(8,128)} %get-tuple-element.49.conv_ref, f32[2048,768]{1,0:T(8,128)} %get-tuple-element.50.scanned_ref, ...), custom_call_target="tpu_custom_call" | custom-call | flops 3221225472 | bytes 56623104 | tf_op jit(solution)/shard_map/mixer_backward/pallas_call | solution.py:337
  342.8 20.4 %fusion.55 = (bf16[1536,1920]{1,0:T(8,128)(2,1)}, f32[1536]{0:T(1024)}) fusion(bf16[1536,1920]{1,0:T(8,128)(2,1)} %all-gather.7.cloned.1.call-done, bf16[2048,1920]{1,0:T(8,128)(2,1)} %get-tuple-element.52, bf16[2048,1,1536]{2,0,1:T(8,128)(2,1)} %all-gather.5.cloned.1.call-done), kind=kOutput, calls=%fused_computation.107 | convolution fusion | flops 12091389952 | bytes 25958400 | tf_op jit(solution)/shard_map/dot_general | solution.py:519
  363.5 10.4 %fusion.23 = bf16[1536,768]{0,1:T(8,128)(2,1)} fusion(bf16[2048,1,1536]{2,0,1:T(8,128)(2,1)} %all-gather.9.cloned.1.call-done, f32[2048,768]{1,0:T(8,128)} %get-tuple-element.47, f32[2048]{0:T(1024)S(1)} %bitcast.51, f32[768]{0:T(1024)S(1)} %copy-done.19), kind=kOutput, calls=%fused_computation.30 | convolution fusion | flops 4837736448 | bytes 14953472 | tf_op jit(solution)/shard_map/dot_general | solution.py:519
  373.9 4.3 copy.192
  378.3 51.1 %reduce-scatter.16.cloned.1.call-done = bf16[192,1920]{1,0:T(8,128)(2,1)} async-done(((bf16[1536,1920]{1,0:T(8,128)(2,1)}), bf16[192,1920]{1,0:T(8,128)(2,1)}) %reduce-scatter.16.cloned.1.call-update) | async-done | bytes 737296
  432.2 18.5 %fusion = bf16[2048,1,1536]{2,0,1:T(8,128)(2,1)} fusion(bf16[2048,1920]{1,0:T(8,128)(2,1)} %get-tuple-element.52, bf16[1536,1920]{1,0:T(8,128)(2,1)} %all-gather.7.cloned.1.call-done), kind=kOutput, calls=%fused_computation.3 | convolution fusion | flops 12082741248 | bytes 20054016 | tf_op jit(solution)/shard_map/dot_general | solution.py:30
  450.8 10.3 %fusion.1 = bf16[2048,1,1536]{2,0,1:T(8,128)(2,1)} fusion(bf16[1536,768]{1,0:T(8,128)(2,1)} %all-gather.11.cloned.1.call-done, f32[2048,768]{1,0:T(8,128)} %get-tuple-element.47, f32[2048]{0:T(1024)S(1)} %bitcast.52, f32[768]{0:T(1024)S(1)} %copy-done.19), kind=kOutput, calls=%fused_computation.4 | convolution fusion | flops 4839702528 | bytes 14953472 | tf_op jit(solution)/shard_map/dot_general | solution.py:30
  476.1 38.7 %all-reduce.2 = (f32[1536]{0:T(1024)}, f32[5,256]{1,0:T(8,128)}) all-reduce(f32[1536]{0:T(1024)} %div.172, f32[5,256]{1,0:T(8,128)} %slice.62), channel_id=1, replica_groups=mesh['dp'=8,'tensor'=4] {'dp','tensor'}, use_global_device_ids=true, to_apply=%region_7.8 | all-reduce | flops 2816 | bytes 22528 | tf_op jit(solution)/shard_map/psum | solution.py:495
  516.1 29.8 %all-reduce.3 = (f32[5,768]{1,0:T(8,128)}, f32[3,12]{1,0:T(4,128)}, f32[768]{0:T(1024)}) all-reduce(f32[5,768]{1,0:T(8,128)} %slice.61, f32[3,12]{1,0:T(4,128)} %pad_maximum_fusion.3, f32[768]{0:T(1024)} %get-tuple-element.246), channel_id=1, replica_groups=mesh['dp'=8,'tensor'=4] {'dp'}, use_global_device_ids=true, to_apply=%region_10.11 | all-reduce | flops 4644 | bytes 37152 | tf_op jit(solution)/shard_map/psum | solution.py:494
  552.8 3.1 multiply_subtract_fusion.1
  557.3 3.2 multiply_subtract_fusion
  560.5 3.0 copy.181
  565.0 3.0 copy.185
  581.2 59.2 %reduce-scatter.12.cloned.1.call-done = bf16[512,1,1536]{2,0,1:T(8,128)(2,1)} async-done(((bf16[2048,1,1536]{2,0,1:T(8,128)(2,1)}), bf16[512,1,1536]{2,0,1:T(8,128)(2,1)}) %reduce-scatter.12.cloned.1.call-update) | async-done | bytes 1572880 | tf_op jit(solution)/shard_map/reduce_scatter | solution.py:450
  640.4 4.3 fusion.20
  644.7 4.9 copy.178
  (123 shorter events, 56.4 us)
Async XLA Ops:
  7.2 5.0 copy-start.13
  7.2 5.1 copy-start.11
  7.2 5.2 copy-start.5
  7.3 77.9 %all-gather.5.cloned.1.call-start = ((), (), s32[]{:S(2)}) async-start(), calls=%async_computation.5 | async-start | bytes 7864320 | tf_op jit(solution)/shard_map/all_gather | solution.py:413
  12.2 11.4 %copy-start.8 = (f32[768,192]{0,1:T(8,128)S(1)}, f32[768,192]{0,1:T(8,128)}, u32[]{:S(2)}) copy-start(f32[768,192]{0,1:T(8,128)} %param.39) | copy-start | bytes 1769476
  12.2 136.6 %all-gather.7.cloned.1.call-start = ((), (), s32[]{:S(2)}) async-start(), calls=%async_computation.6 | async-start | bytes 6635520 | tf_op jit(solution)/shard_map/all_gather | solution.py:423
  12.5 12.4 %copy-start.19 = (f32[768]{0:T(1024)S(1)}, f32[768]{0:T(1024)}, u32[]{:S(2)}) copy-start(f32[768]{0:T(1024)} %param.38) | copy-start | bytes 9220
  12.5 13.0 %copy-start.20 = (f32[3,12]{1,0:T(4,128)S(1)}, f32[3,12]{1,0:T(4,128)}, u32[]{:S(2)}) copy-start(f32[3,12]{1,0:T(4,128)} %param.37) | copy-start | bytes 436
  12.5 14.3 %copy-start.12 = (f32[5,768]{1,0:T(8,128)S(1)}, f32[5,768]{1,0:T(8,128)}, u32[]{:S(2)}) copy-start(f32[5,768]{1,0:T(8,128)} %param.35) | copy-start | bytes 46084
  22.5 4.4 copy-start.16
  23.5 175.3 %all-gather.11.cloned.1.call-start = ((), (), s32[]{:S(2)}) async-start(), calls=%async_computation.8 | async-start | bytes 2654208 | tf_op jit(solution)/shard_map/all_gather | solution.py:424
  24.3 227.9 %all-gather.9.cloned.1.call-start = ((), (), s32[]{:S(2)}) async-start(), calls=%async_computation.7 | async-start | bytes 7864320 | tf_op jit(solution)/shard_map/all_gather | solution.py:425
  24.9 404.5 %reduce-scatter.16.cloned.1.call-start = ((), (), s32[]{:S(2)}) async-start(), calls=%async_computation.11 | async-start | bytes 6635520
  26.9 141.1 %copy-start.9 = (f32[5,1024]{1,0:T(8,128)}, f32[5,1024]{1,0:T(8,128)S(1)}, u32[]{:S(2)}) copy-start(f32[5,1024]{1,0:T(8,128)S(1)} %constant_dynamic-update-slice_fusion.taps_ref) | copy-start | bytes 61444
  363.3 189.5 %reduce-scatter.20.cloned.1.call-start = ((), (), s32[]{:S(2)}) async-start(), calls=%async_computation.13 | async-start | bytes 2654208 | tf_op jit(solution)/shard_map/reduce_scatter | solution.py:457
  378.2 192.7 %reduce-scatter.18.cloned.1.call-start = ((), (), s32[]{:S(2)}) async-start(), calls=%async_computation.12 | async-start | bytes 245760
  431.1 19.6 %copy-start.6 = (bf16[192,1920]{0,1:T(8,128)(2,1)}, bf16[192,1920]{0,1:T(8,128)(2,1)S(1)}, u32[]{:S(2)}) copy-start(bf16[192,1920]{0,1:T(8,128)(2,1)S(1)} %copy.189) | copy-start | bytes 2211844
  432.2 146.9 %reduce-scatter.14.cloned.1.call-start = ((), (), s32[]{:S(2)}) async-start(), calls=%async_computation.10 | async-start | bytes 7864320 | tf_op jit(solution)/shard_map/reduce_scatter | solution.py:465
  450.8 189.6 %reduce-scatter.12.cloned.1.call-start = ((), (), s32[]{:S(2)}) async-start(), calls=%async_computation.9 | async-start | bytes 7864320 | tf_op jit(solution)/shard_map/reduce_scatter | solution.py:450
  462.0 8.7 %copy-start.10 = (f32[1536]{0:T(1024)S(1)}, f32[1536]{0:T(1024)}, u32[]{:S(2)}) copy-start(f32[1536]{0:T(1024)} %param.31) | copy-start | bytes 18436
  563.5 4.5 copy-start.2
  565.0 14.1 %copy-start = (bf16[512,1,1536]{2,0,1:T(8,128)(2,1)S(1)}, bf16[512,1,1536]{2,0,1:T(8,128)(2,1)}, u32[]{:S(2)}) copy-start(bf16[512,1,1536]{2,0,1:T(8,128)(2,1)} %param.29) | copy-start | bytes 4718596
  565.0 14.1 %copy-start.18 = (f32[512]{0:T(512)S(1)}, f32[512]{0:T(512)}, u32[]{:S(2)}) copy-start(f32[512]{0:T(512)} %copy-done.17) | copy-start | bytes 6148
  569.4 70.9 %copy-start.4 = (bf16[512,1,1536]{2,0,1:T(8,128)(2,1)S(1)}, bf16[512,1,1536]{2,0,1:T(8,128)(2,1)}, u32[]{:S(2)}) copy-start(bf16[512,1,1536]{2,0,1:T(8,128)(2,1)} %param.30) | copy-start | bytes 4718596
  (6 other events, 12.3 us)
Sparse Core Ops, SparseCore 0:
  12.3 72.7 all-gather.4
  87.3 61.4 all-gather.6
  151.0 30.1 all-gather.10
  182.9 69.2 all-gather.8
  363.4 65.9 reduce-scatter.15
  431.6 35.5 reduce-scatter.19
  470.5 23.0 reduce-scatter.17
  496.6 70.6 reduce-scatter.13
  570.3 70.0 reduce-scatter.11

commit v2 on v1

--- a/solution.py
+++ b/solution.py
@@ -42,6 +42,265 @@
     return mm(high, weight) + mm(low, weight)
 
 
+MESH = pl.DeviceIdType.MESH
+
+
+def meet(peers, beside=()):
+    barrier = pltpu.get_barrier_semaphore()
+    for peer in peers:
+        pl.semaphore_signal(barrier, inc=1, device_id={"dp": peer}, device_id_type=MESH)
+    for peer in beside:
+        pl.semaphore_signal(barrier, inc=1, device_id={"tensor": peer}, device_id_type=MESH)
+    pl.semaphore_wait(barrier, len(peers) + len(beside))
+
+
+def send(source, target, send_sem, recv_sem, peer, axis="dp"):
+    return pltpu.make_async_remote_copy(
+        src_ref=source,
+        dst_ref=target,
+        send_sem=send_sem,
+        recv_sem=recv_sem,
+        device_id={axis: peer},
+        device_id_type=MESH,
+    )
+
+
+def gather_kernel(n, own_ref, full_ref, own_sem, far_send, far_recv, near_send, near_recv):
+    rows = own_ref.shape[0]
+    chips = n // 2
+    me = lax.axis_index("dp")
+    core = lax.rem(me, 2)
+    chip = me // 2
+    partner = me + 1 - 2 * core
+    others = [2 * lax.rem(chip + 1 + k, chips) + core for k in range(chips - 1)]
+    meet(others + [partner])
+
+    def place(index):
+        return full_ref.at[pl.ds(pl.multiple_of(index * rows, rows), rows), :]
+
+    far = [
+        send(own_ref, place(me), far_send.at[k], far_recv.at[k], others[k]) for k in range(chips - 1)
+    ]
+    for copy in far:
+        copy.start()
+    near = [send(own_ref, place(me), near_send.at[chips - 1], near_recv.at[chips - 1], partner)]
+    near[0].start()
+    kept = pltpu.make_async_copy(own_ref, place(me), own_sem)
+    kept.start()
+    for k in range(chips - 1):
+        source = 2 * lax.rem(chip + chips - 1 - k, chips) + core
+        far[k].wait_recv()
+        copy = send(place(source), place(source), near_send.at[k], near_recv.at[k], partner)
+        copy.start()
+        near.append(copy)
+    kept.wait()
+    for copy in far:
+        copy.wait_send()
+    for copy in near:
+        copy.wait()
+
+
+def gather_dp(own, n):
+    rows, cols = own.shape
+    return pl.pallas_call(
+        functools.partial(gather_kernel, n),
+        out_shape=jax.ShapeDtypeStruct((rows * n, cols), own.dtype),
+        in_specs=[pl.BlockSpec(memory_space=pltpu.VMEM)],
+        out_specs=pl.BlockSpec(memory_space=pl.ANY),
+        scratch_shapes=[
+            pltpu.SemaphoreType.DMA(()),
+            pltpu.SemaphoreType.DMA((n // 2 - 1,)),
+            pltpu.SemaphoreType.DMA((n // 2 - 1,)),
+            pltpu.SemaphoreType.DMA((n // 2,)),
+            pltpu.SemaphoreType.DMA((n // 2,)),
+        ],
+        compiler_params=pltpu.CompilerParams(collective_id=0, has_side_effects=True),
+        cost_estimate=pl.CostEstimate(flops=0, bytes_accessed=240_000_000, transcendentals=0),
+        name="gather_dp",
+    )(own)
+
+
+class Exchange:
+    def __init__(self, n, terms, near_buf, out_buf, far_buf, near_send, near_recv, far_send, far_recv):
+        self.n, self.terms, self.near_buf, self.out_buf, self.far_buf = n, terms, near_buf, out_buf, far_buf
+        self.near_send, self.near_recv, self.far_send, self.far_recv = near_send, near_recv, far_send, far_recv
+        self.chips = n // 2
+        self.rows = terms.shape[0] // n
+        me = lax.axis_index("dp")
+        self.core = lax.rem(me, 2)
+        self.partner = me + 1 - 2 * self.core
+        self.order = [lax.rem(me // 2 + 1 + k, self.chips) for k in range(self.chips)]
+
+    def block(self, index):
+        return pl.ds(pl.multiple_of(index * self.rows, self.rows), self.rows)
+
+    def near(self, k):
+        index = 2 * self.order[k] + 1 - self.core
+        return send(
+            self.terms.at[self.block(index), :], self.near_buf.at[k],
+            self.near_send.at[k], self.near_recv.at[k], self.partner,
+        )
+
+    def far(self, k):
+        return send(
+            self.out_buf.at[k], self.far_buf.at[k],
+            self.far_send.at[k], self.far_recv.at[k], 2 * self.order[k] + self.core,
+        )
+
+    def start(self):
+        for k in range(self.chips):
+            self.near(k).start()
+
+    def pair_sum(self, k):
+        return self.terms[self.block(2 * self.order[k] + self.core), :] + self.near_buf[k]
+
+    def forward(self):
+        for k in range(self.chips - 1):
+            self.near(k).wait()
+            self.out_buf[k] = self.pair_sum(k).astype(bf16)
+            self.far(k).start()
+
+    def finish(self):
+        self.near(self.chips - 1).wait()
+        total = self.pair_sum(self.chips - 1)
+        for k in range(self.chips - 1):
+            self.far(k).wait()
+            total = total + self.far_buf[k].astype(f32)
+        return total
+
+    @staticmethod
+    def scratch(n, rows, cols):
+        chips = n // 2
+        return [
+            pltpu.VMEM((chips, rows, cols), f32),
+            pltpu.VMEM((chips - 1, rows, cols), bf16),
+            pltpu.VMEM((chips - 1, rows, cols), bf16),
+            pltpu.SemaphoreType.DMA((chips,)),
+            pltpu.SemaphoreType.DMA((chips,)),
+            pltpu.SemaphoreType.DMA((chips - 1,)),
+            pltpu.SemaphoreType.DMA((chips - 1,)),
+        ]
+
+
+def all_others(n, axis="dp"):
+    me = lax.axis_index(axis)
+    return [lax.rem(me + 1 + k, n) for k in range(n - 1)]
+
+
+def sum_kernel(
+    n, shards, start, terms_ref, small_ref, own_ref, small_out_ref, shared_ref, state_ref, *scratch
+):
+    small_buf, small_send, small_recv, state_out, state_buf, shared_buf = scratch[7:13]
+    state_send, state_recv, shared_send, shared_recv = scratch[13:]
+    others = all_others(n)
+    beside = all_others(shards, "tensor")
+    meet(others, beside)
+    exchange = Exchange(n, terms_ref, *scratch[:7])
+    exchange.start()
+    copies = [
+        send(small_ref, small_buf.at[k], small_send.at[k], small_recv.at[k], others[k])
+        for k in range(n - 1)
+    ]
+    for copy in copies:
+        copy.start()
+    exchange.forward()
+    small = small_ref[...]
+    for k in range(n - 1):
+        copies[k].wait()
+        small = small + small_buf[k]
+    small_out_ref[...] = small
+    own_ref[...] = exchange.finish()
+    rows, cols = state_ref.shape
+    for k in range(shards):
+        state_out[k] = own_ref[k * rows : (k + 1) * rows, start : start + cols]
+    shared = [
+        send(small_out_ref, shared_buf.at[k], shared_send.at[k], shared_recv.at[k], beside[k], "tensor")
+        for k in range(shards - 1)
+    ]
+    parts = [
+        send(
+            state_out.at[beside[k]], state_buf.at[k], state_send.at[k], state_recv.at[k], beside[k], "tensor"
+        )
+        for k in range(shards - 1)
+    ]
+    for copy in shared + parts:
+        copy.start()
+    total = state_out[lax.axis_index("tensor")]
+    for k in range(shards - 1):
+        shared[k].wait()
+        small = small + shared_buf[k]
+    shared_ref[...] = small
+    for k in range(shards - 1):
+        parts[k].wait()
+        total = total + state_buf[k]
+    state_ref[...] = total
+
+
+def sum_dp(terms, small, n, shards, start, states):
+    rows, cols = terms.shape[0] // n, terms.shape[1]
+    part = (rows // shards, states)
+    vmem = pl.BlockSpec(memory_space=pltpu.VMEM)
+    return pl.pallas_call(
+        functools.partial(sum_kernel, n, shards, start),
+        out_shape=[
+            jax.ShapeDtypeStruct((rows, cols), f32),
+            jax.ShapeDtypeStruct(small.shape, f32),
+            jax.ShapeDtypeStruct(small.shape, f32),
+            jax.ShapeDtypeStruct(part, f32),
+        ],
+        in_specs=[vmem, vmem],
+        out_specs=[vmem, vmem, vmem, vmem],
+        scratch_shapes=Exchange.scratch(n, rows, cols)
+        + [
+            pltpu.VMEM((n - 1,) + small.shape, f32),
+            pltpu.SemaphoreType.DMA((n - 1,)),
+            pltpu.SemaphoreType.DMA((n - 1,)),
+            pltpu.VMEM((shards,) + part, f32),
+            pltpu.VMEM((shards - 1,) + part, f32),
+            pltpu.VMEM((shards - 1,) + small.shape, f32),
+        ]
+        + [pltpu.SemaphoreType.DMA((shards - 1,))] * 4,
+        compiler_params=pltpu.CompilerParams(
+            collective_id=1, has_side_effects=True, vmem_limit_bytes=56 * 1024 * 1024
+        ),
+        cost_estimate=pl.CostEstimate(flops=0, bytes_accessed=240_000_000, transcendentals=0),
+        name="sum_dp",
+    )(terms, small)
+
+
+def token_kernel(shards, own_ref, total_ref, buf, send_sem, recv_sem):
+    beside = all_others(shards, "tensor")
+    meet((), beside)
+    copies = [
+        send(own_ref, buf.at[k], send_sem.at[k], recv_sem.at[k], beside[k], "tensor")
+        for k in range(shards - 1)
+    ]
+    for copy in copies:
+        copy.start()
+    total = own_ref[...]
+    for k in range(shards - 1):
+        copies[k].wait()
+        total = total + buf[k]
+    total_ref[...] = total
+
+
+def sum_tensor(own, shards):
+    vmem = pl.BlockSpec(memory_space=pltpu.VMEM)
+    return pl.pallas_call(
+        functools.partial(token_kernel, shards),
+        out_shape=jax.ShapeDtypeStruct(own.shape, f32),
+        in_specs=[vmem],
+        out_specs=vmem,
+        scratch_shapes=[
+            pltpu.VMEM((shards - 1,) + own.shape, f32),
+            pltpu.SemaphoreType.DMA((shards - 1,)),
+            pltpu.SemaphoreType.DMA((shards - 1,)),
+        ],
+        compiler_params=pltpu.CompilerParams(collective_id=3, has_side_effects=True),
+        name="sum_tensor",
+    )(own)
+
+
 def sigmoid(v):
     return 1.0 / (1.0 + jnp.exp(-v))
 
@@ -63,7 +322,7 @@
 
 def forward_kernel(
     width, size, pre_ref, taps_ref, heads_ref, skip_ref, spread_ref,
-    scanned_ref, conv_ref, gated_ref, squares_ref, states_ref,
+    scanned_ref, conv_ref, gated_ref, states_ref,
     ext, state, act,
 ):
     count = pre_ref.shape[0]
@@ -89,7 +348,7 @@
         act[:, cols] = total * sigmoid(total)
         ext[0:CARRY, cols] = ext[count : count + CARRY, cols]
 
-    shifted, steps, logs, cumul = step_terms(pre_ref[:, width + conv_width :], heads_ref)
+    _, steps, _, cumul = step_terms(pre_ref[:, width + conv_width :], heads_ref)
     cumul_t = cumul.T
     final = cumul[count - 1 : count, :]
     decay_in = jnp.exp(cumul)
@@ -100,7 +359,6 @@
     scores = mm_nt(queries, keys)
     causal = tri_lower(half)
     lane = lax.broadcasted_iota(jnp.int32, (count, LANES), 1)
-    squares = jnp.zeros((count, LANES), f32)
     for tile in range(width // LANES):
         cols = slice(tile * LANES, (tile + 1) * LANES)
         spread = spread_ref[:, cols]
@@ -128,16 +386,28 @@
         gate = pre_ref[:, cols]
         gated = (scanned + skip_ref[:, cols] * inner) * (gate * sigmoid(gate))
         gated_ref[:, cols] = gated
-        squares = squares + gated * gated
-    squares_ref[...] = jnp.sum(squares, axis=1, keepdims=True)
 
 
 def backward_kernel(
-    width, size, pre_ref, conv_ref, scanned_ref, dnormed_ref, token_ref, states_ref,
-    taps_ref, heads_ref, skip_ref, gain_ref, spread_ref, gather_ref,
-    dpre_ref, taps_grad_ref, wide_grad_ref, heads_grad_ref,
-    ext, dstate, dscores, in_rows, out_rows, dstate_b, finals,
+    n, width, size, pre_ref, conv_ref, scanned_ref, dnormed_ref, token_ref, states_ref,
+    taps_ref, heads_ref, skip_ref, gain_ref, spread_ref, gather_ref, terms_ref,
+    dpre_ref, taps_grad_ref, wide_grad_ref, heads_grad_ref, own_ref,
+    ext, dstate, dscores, in_rows, out_rows, dstate_b, finals, *scratch,
 ):
+    exchange = Exchange(n, terms_ref, *scratch)
+    opening = (pl.program_id(0) == 0) & (pl.program_id(1) == 0)
+    middle = (pl.program_id(0) == 0) & (pl.program_id(1) == 1)
+    closing = (pl.program_id(0) == pl.num_programs(0) - 1) & (pl.program_id(1) == pl.num_programs(1) - 1)
+
+    @pl.when(opening)
+    def _():
+        meet(all_others(n))
+        exchange.start()
+
+    @pl.when(middle)
+    def _():
+        exchange.forward()
+
     count = pre_ref.shape[0]
     half = count // 2
     conv_width = taps_ref.shape[1]
@@ -150,7 +420,7 @@
         ext[count : count + CARRY, :] = jnp.zeros((CARRY, conv_width), f32)
         dstate[...] = jnp.zeros_like(dstate)
 
-    @pl.when((pl.program_id(0) == 0) & (pl.program_id(1) == 0))
+    @pl.when(opening)
     def _():
         taps_grad_ref[...] = jnp.zeros_like(taps_grad_ref)
         wide_grad_ref[...] = jnp.zeros_like(wide_grad_ref)
@@ -282,6 +552,10 @@
     heads_grad_ref[0:1, :] += jnp.sum(dlogs * logs, axis=0, keepdims=True)
     heads_grad_ref[1:2, :] += jnp.sum(dshifted, axis=0, keepdims=True)
 
+    @pl.when(closing)
+    def _():
+        own_ref[...] = exchange.finish()
+
 
 def whole(shape):
     return pl.BlockSpec(shape, lambda s, i: (0,) * len(shape))
@@ -302,14 +576,13 @@
         grid=(seqs, blocks),
         in_specs=[block(cat), whole(taps.shape), whole(heads.shape), whole(skip.shape), whole(spread.shape)],
         out_specs=[
-            block(width), block(conv_width), block(width), block(1),
+            block(width), block(conv_width), block(width),
             pl.BlockSpec((1, state_size, width), lambda s, i: (s * blocks + i, 0, 0)),
         ],
         out_shape=[
             jax.ShapeDtypeStruct((rows, width), f32),
             jax.ShapeDtypeStruct((rows, conv_width), f32),
             jax.ShapeDtypeStruct((rows, width), f32),
-            jax.ShapeDtypeStruct((rows, 1), f32),
             jax.ShapeDtypeStruct((seqs * blocks, state_size, width), f32),
         ],
         scratch_shapes=[
@@ -324,7 +597,7 @@
     )(pre, taps, heads, skip, spread)
 
 
-def run_backward(pre, conv, scanned, dnormed, token, states, taps, heads, skip, gain, spread, gather, seqs, count, size):
+def run_backward(pre, conv, scanned, dnormed, token, states, taps, heads, skip, gain, spread, gather, terms, n, seqs, count, size):
     rows, cat = pre.shape
     width = skip.shape[1]
     conv_width = taps.shape[1]
@@ -335,20 +608,25 @@
         return pl.BlockSpec((count, cols), lambda s, i: (s * blocks + blocks - 1 - i, 0))
 
     return pl.pallas_call(
-        functools.partial(backward_kernel, width, size),
+        functools.partial(backward_kernel, n, width, size),
         grid=(seqs, blocks),
         in_specs=[
             block(cat), block(conv_width), block(width), block(width), block(2),
             pl.BlockSpec((1, state_size, width), lambda s, i: (s * blocks + blocks - 1 - i, 0, 0)),
             whole(taps.shape), whole(heads.shape), whole(skip.shape), whole(gain.shape),
             whole(spread.shape), whole(gather.shape),
-        ],
-        out_specs=[block(cat), whole((8, conv_width)), whole((8, width)), whole((8, LANES))],
+            pl.BlockSpec(memory_space=pltpu.VMEM),
+        ],
+        out_specs=[
+            block(cat), whole((8, conv_width)), whole((8, width)), whole((8, LANES)),
+            whole((terms.shape[0] // n, terms.shape[1])),
+        ],
         out_shape=[
             jax.ShapeDtypeStruct((rows, cat), bf16),
             jax.ShapeDtypeStruct((8, conv_width), f32),
             jax.ShapeDtypeStruct((8, width), f32),
             jax.ShapeDtypeStruct((8, LANES), f32),
+            jax.ShapeDtypeStruct((terms.shape[0] // n, terms.shape[1]), f32),
         ],
         scratch_shapes=[
             pltpu.VMEM((count + CARRY, conv_width), f32),
@@ -358,12 +636,16 @@
             pltpu.VMEM((count, width), bf16),
             pltpu.VMEM((state_size, width), bf16),
             pltpu.VMEM((8, width), f32),
-        ],
+        ]
+        + Exchange.scratch(n, terms.shape[0] // n, terms.shape[1]),
+        compiler_params=pltpu.CompilerParams(
+            collective_id=2, has_side_effects=True, vmem_limit_bytes=56 * 1024 * 1024
+        ),
         cost_estimate=pl.CostEstimate(
             flops=rows * width * count * 8, bytes_accessed=rows * (2 * cat + 4 * width) * 4, transcendentals=rows * count * 12
         ),
         name="mixer_backward",
-    )(pre, conv, scanned, dnormed, token, states, taps, heads, skip, gain, spread, gather)
+    )(pre, conv, scanned, dnormed, token, states, taps, heads, skip, gain, spread, gather, terms)
 
 
 def adam_step(param, first, second_moment, grad, rate):
@@ -388,14 +670,12 @@
         gated_gain,
         output_matrix,
     ) = params
-    local_len, seqs, features = hidden.shape
+    _, seqs, features = hidden.shape
     wide = inner_taps.shape[1]
     heads = head_params.shape[1]
     size = wide // heads
     states = state_taps.shape[1]
     shards = lax.axis_size("tensor")
-    length = local_len * shards
-    rows = length * seqs
     inner_total = wide * shards
 
     base = hidden.astype(f32)
@@ -420,8 +700,13 @@
         ],
         axis=1,
     )
-    weights = lax.all_gather(weights_own, "dp", axis=0, tiled=True)
-    output_t = lax.all_gather(output_matrix.astype(bf16).T, "dp", axis=0, tiled=True)
+    replicas = lax.axis_size("dp")
+    gathered = gather_dp(
+        jnp.concatenate([weights_own, output_matrix.astype(bf16).T], axis=1), replicas
+    )
+    cat = weights_own.shape[1]
+    weights = gathered[:, :cat]
+    output_t = gathered[:, cat:]
     full_cot = lax.all_gather(cotangent, "tensor", axis=0, tiled=True)
     flat_in = by_sequence(full_in)
     flat_cot = by_sequence(full_cot)
@@ -436,49 +721,49 @@
     gather = (jnp.arange(wide)[:, None] // size == jnp.arange(LANES)[None]).astype(bf16)
 
     pre = mm(flat_in, weights)
-    scanned, conv, gated, squares, chunk_states = run_forward(
+    scanned, conv, gated, chunk_states = run_forward(
         pre, taps, head_rows, skip, spread, seqs, GROUP, size
     )
     d_normed = mm(flat_cot, output_t)
-    crossed = jnp.sum(d_normed * gain * gated, -1, keepdims=True)
-    sums = lax.psum(jnp.concatenate([squares, crossed], axis=1), "tensor")
-    scale = lax.rsqrt(sums[:, 0:1] / inner_total + norm_eps)
-    token = jnp.concatenate(
-        [scale, scale * scale * scale * (sums[:, 1:2] / inner_total)], axis=1
-    )
+    sums = sum_tensor(
+        jnp.stack([jnp.sum(gated * gated, -1), jnp.sum(d_normed * gain * gated, -1)]), shards
+    )
+    scale_row = lax.rsqrt(sums[0] / inner_total + norm_eps)
+    token = jnp.stack([scale_row, scale_row**3 * (sums[1] / inner_total)], axis=1)
+    scale = token[:, 0:1]
     normed_out = (gated * scale * gain).astype(bf16)
-    branch = lax.psum_scatter(
-        by_position(mm_nt(normed_out, output_t)).astype(bf16),
-        "tensor",
-        scatter_dimension=0,
-        tiled=True,
-    )
+    branch_part = by_position(mm_nt(normed_out, output_t)).astype(bf16)
+    branch_part, d_normed = lax.optimization_barrier((branch_part, d_normed))
+    branch = lax.psum_scatter(branch_part, "tensor", scatter_dimension=0, tiled=True)
     result = (base + branch.astype(f32)).astype(bf16)
-    grad_output_t = lax.psum_scatter(
-        contract_first(flat_cot, normed_out).astype(bf16), "dp", scatter_dimension=0, tiled=True
-    )
-
-    d_pre, taps_grad, wide_grad, head_grad = run_backward(
+    output_terms = contract_first(flat_cot, normed_out)
+
+    d_pre, taps_grad, wide_grad, head_grad, grad_output_t = run_backward(
         pre, conv, scanned, d_normed, token, chunk_states, taps, head_rows, skip, gain,
-        spread, gather, seqs, GROUP, size,
-    )
+        spread, gather, output_terms, replicas, seqs, GROUP, size,
+    )
+    d_in_part = mm_nt(d_pre, weights)
     d_in = lax.psum_scatter(
-        by_position(mm_nt(d_pre, weights)).astype(bf16),
-        "tensor",
-        scatter_dimension=0,
-        tiled=True,
+        by_position(d_in_part.astype(bf16)), "tensor", scatter_dimension=0, tiled=True
     ).astype(f32)
-    grad_weights = contract_first(flat_in, d_pre)
-    grad_own = lax.psum_scatter(
-        grad_weights.astype(bf16), "dp", scatter_dimension=0, tiled=True
-    )
-    grad_gain_rows = jnp.sum(grad_weights * weights.astype(f32), axis=1) / input_gain
-    grad_state = lax.psum_scatter(
-        grad_own[:, 2 * wide : 2 * wide + states].astype(f32),
-        "tensor",
-        scatter_dimension=0,
-        tiled=True,
-    )
+    grad_gain_rows = jnp.sum(d_in_part * flat_in.astype(f32), axis=0) / input_gain
+    gain_cols = -(-features // (8 * LANES)) * LANES
+    small = jnp.concatenate(
+        [
+            taps_grad,
+            wide_grad,
+            head_grad,
+            jnp.pad(grad_gain_rows, (0, 8 * gain_cols - features)).reshape(8, gain_cols),
+        ],
+        axis=1,
+    )
+    grad_own, small_sums, shared_sums, grad_state = sum_dp(
+        contract_first(flat_in, d_pre), small, replicas, shards, 2 * wide, states
+    )
+    taps_grad = small_sums[:, : wide + states]
+    wide_grad = small_sums[:, wide + states : 2 * wide + states]
+    head_grad = small_sums[:, 2 * wide + states : 2 * wide + states + LANES]
+    grad_gain_rows = shared_sums[:, 2 * wide + states + LANES :].reshape(-1)[:features]
 
     d_hat = d_in * input_gain
     gradient_hidden = cotangent.astype(f32) + rstd * (
@@ -490,20 +775,17 @@
         jnp.concatenate([head_grad[:2, :heads], grad_skip[None]], axis=0),
         wide_grad[0],
     )
-    shared_terms = (grad_gain_rows, taps_grad[: state_taps.shape[0], wide:])
-    split_sums = lax.psum(split_terms, "dp")
-    shared_sums = lax.psum(shared_terms, ("dp", "tensor"))
-    own = grad_own.astype(f32)
+    own = grad_own
     grads = (
-        shared_sums[0],
+        grad_gain_rows,
         jnp.stack([own[:, :wide], own[:, wide : 2 * wide]]),
         own[:, 2 * wide + states : 2 * wide + states + heads],
         grad_state,
-        split_sums[0],
-        shared_sums[1],
-        split_sums[1],
-        split_sums[2],
-        grad_output_t.astype(f32).T,
+        split_terms[0],
+        shared_sums[: state_taps.shape[0], wide : wide + states],
+        split_terms[1],
+        split_terms[2],
+        grad_output_t.T,
     )
     stepped = [
         adam_step(param, first, second_moment, grad, rate)
@@ -532,6 +814,7 @@
         P("tensor", "dp"),
     )
     rows = P("tensor", "dp", None)
+
     return jax.shard_map(
         body,
         mesh=mesh,

time: 665 us -> 476 us (0.72)
  waiting for transfers between devices: 285 us -> 23.5 us
  Pallas kernels: 92.3 us -> 282 us
  blocking collectives: 93.8 us -> 9.84 us
  local copies, waits for them, and re-layouts: 45.2 us -> 17.5 us
  other arithmetic: 35.7 us -> 28.1 us
    pallas_call x1 -> x4, Pallas kernels: 63.1 us -> 253 us  [the longest x1 86.9 us: run_backward(): pl.pallas_call(functools.partial(backward_kernel, n, width, size), grid=(...]
    psum x3 -> x0, blocking collectives: 83.9 us -> none  [the longest x1 38.7 us: body(): shared_sums = lax.psum(shared_terms, ('dp', 'tensor'))]
    all_gather x2 -> x0, waiting for transfers between devices: 63.7 us -> none  [the longest x1 63.7 us: body(): weights = lax.all_gather(weights_own, 'dp', axis=0, tiled=True)]
    all_gather x1, waiting for transfers between devices: 56.6 us -> 0.01 us  [body(): full_in = lax.all_gather(normed_in, 'tensor', axis=0, tiled=True)]
    unnamed x11 -> x4, waiting for transfers between devices: 51.8 us -> 1.25 us
    all_gather x1, waiting for transfers between devices: 53.4 us -> 3.62 us  [body(): full_cot = lax.all_gather(cotangent, 'tensor', axis=0, tiled=True)]
    reduce_scatter x3 -> x2, waiting for transfers between devices: 59.2 us -> 18.6 us  [the longest x1 18.6 us: body(): lax.psum_scatter(branch_part, 'tensor', scatter_dimension=0, tiled=True)]
    unnamed x62 -> x113, local copies, waits for them, and re-layouts: 34.2 us -> 10.5 us
  transfers between devices with their start and end apart: 9 -> 4, of which waited for: 5 -> 2; matrix products, arithmetic and copies ran while one was open for 19% -> 14% of each run, Pallas kernels for 4% -> 41%
where the time goes in v2:
time: 476 us; the launch traced here: 467 us
  Pallas kernels  282 us (59%)
  matrix products  90.8 us (19%)
  other arithmetic  28.1 us (6%)
  waiting for transfers between devices  23.5 us (5%)
  local copies, waits for them, and re-layouts  17.5 us (4%)
  between operations  14.7 us (3%)
  blocking collectives  9.84 us (2%)
    pallas_call x1, Pallas kernels, run_backward(): pl.pallas_call(functools.partial(backward_kernel, n, width, size), grid=(...  86.9 us
    pallas_call x1, Pallas kernels, sum_dp(): pl.pallas_call(functools.partial(sum_kernel, n, shards, start), out_shape...  83.4 us
    pallas_call x1, Pallas kernels, gather_dp(): pl.pallas_call(functools.partial(gather_kernel, n), out_shape=jax.ShapeDt...  77 us
    dot_general x2, matrix products, contract_first(): lax.dot_general(left, right, (((0,), (0,)), ((), ())), preferred_element_...  32.2 us
    dot_general x2, matrix products, mm(): lax.dot_general(a, b, (((1,), (0,)), ((), ())), preferred_element_type=f32)  29.9 us
    pallas_call x1, Pallas kernels, run_forward(): pl.pallas_call(functools.partial(forward_kernel, width, size), grid=(seqs...  28.9 us
    dot_general x2, matrix products, mm_nt(): lax.dot_general(a, b, (((1,), (1,)), ((), ())), preferred_element_type=f32)  28.7 us
    reduce_scatter x1, waiting for transfers between devices, body(): lax.psum_scatter(branch_part, 'tensor', scatter_dimension=0, tiled=True)  18.6 us
  transfers between devices with their start and end apart: 4, of which 2 were waited for; matrix products, arithmetic and copies ran while one was open for 14% of the time, Pallas kernels for 41%

profile of v2, /device:TPU:0, one launch (start us, length us, event | category | flops | bytes accessed | tf_op | source)
XLA Modules:
  0.0 466.9 jit_solution(13188636425413472942)
XLA Ops:
  7.3 1.8 fusion.26
  9.1 3.1 fusion.21
  15.2 9.8 %all_gather.10 = bf16[192,256]{1,0:T(8,128)(2,1)S(1)} all-gather(bf16[48,256]{1,0:T(8,128)(2,1)S(1)} %convert_element_type.68), channel_id=1, replica_groups=mesh['dp'=8,'tensor'=4] {'tensor'}, dimensions={0}, use_global_device_ids=true | all-gather | bytes 122880 | tf_op jit(solution)/shard_map/all_gather | solution.py:692
  26.2 77.0 %gather_dp.1 = bf16[1536,2688]{1,0:T(8,128)(2,1)} custom-call(bf16[192,2688]{1,0:T(8,128)(2,1)} %copy-done.8), custom_call_target="tpu_custom_call" | custom-call | bytes 240000000 | tf_op jit(solution)/shard_map/gather_dp/pallas_call | solution.py:105
  105.3 19.2 %fusion.7.pre_ref = f32[2048,1920]{1,0:T(8,128)} fusion(bf16[2048,1,1536]{2,0,1:T(8,128)(2,1)} %all-gather.3.cloned.1.call-done, bf16[1536,2688]{1,0:T(8,128)(2,1)} %gather_dp.1), kind=kOutput, calls=%fused_computation.9 | convolution fusion | flops 12079595520 | bytes 27918336 | tf_op jit(solution)/shard_map/dot_general | solution.py:26
  124.5 28.9 %mixer_forward.1 = (f32[2048,768]{1,0:T(8,128)}, f32[2048,1024]{1,0:T(8,128)}, f32[2048,768]{1,0:T(8,128)}, f32[8,128,768]{2,1,0:T(8,128)}) custom-call(f32[2048,1920]{1,0:T(8,128)} %fusion.7.pre_ref, f32[5,1024]{1,0:T(8,128)} %copy-done.13, f32[2,128]{1,0:T(2,128)} %select_maximum_fusion.heads_ref, f32[1,768]{1,0:T(1,128)} %broadcast_in_dim_reshape.3.skip_ref, ...), custom_call_target="tpu_custom_call" | custom-call | flops 1610612736 | bytes 40894464 | tf_op jit(solution)/shard_map/mixer_forward/pallas_call | solution.py:574
  153.4 3.6 all-gather.5.cloned.1.call-done
  157.0 10.7 %multiply_reduce_fusion.2 = (f32[2048]{0:T(1024)S(1)}, f32[2048]{0:T(1024)S(1)}, f32[2048,768]{1,0:T(8,128)}) fusion(f32[2048,768]{1,0:T(8,128)} %get-tuple-element.53, f32[768]{0:T(1024)S(1)} %copy-done.33, bf16[1536,2688]{1,0:T(8,128)(2,1)} %gather_dp.1, bf16[2048,1,1536]{2,0,1:T(8,128)(2,1)} %all-gather.5.cloned.1.call-done), kind=kOutput, calls=%fused_computation.14 | convolution fusion | flops 4839698432 | bytes 21253120 | tf_op jit(solution)/shard_map/dot_general | solution.py:26
  168.4 6.2 %sum_tensor.1 = f32[2,2048]{1,0:T(2,128)} custom-call(f32[2,2048]{1,0:T(2,128)} %pad_maximum_fusion.2.own_ref), custom_call_target="tpu_custom_call" | custom-call | tf_op jit(solution)/shard_map/sum_tensor/pallas_call | solution.py:289
  175.4 10.4 %fusion = bf16[2048,1,1536]{2,0,1:T(8,128)(2,1)} fusion(bf16[1536,2688]{1,0:T(8,128)(2,1)} %gather_dp.1, f32[2048,768]{1,0:T(8,128)} %get-tuple-element.53, f32[2048]{0:T(1024)S(1)} %bitcast.56, f32[768]{0:T(1024)S(1)} %copy-done.33), kind=kOutput, calls=%fused_computation.2 | convolution fusion | flops 4839702528 | bytes 14953472 | tf_op jit(solution)/shard_map/dot_general | solution.py:30
  187.1 11.5 %fusion.18.terms_ref = f32[1536,768]{1,0:T(8,128)} fusion(bf16[2048,1,1536]{2,0,1:T(8,128)(2,1)} %all-gather.5.cloned.1.call-done, f32[2048,768]{1,0:T(8,128)} %get-tuple-element.53, f32[2048]{0:T(1024)S(1)} %bitcast.58, f32[768]{0:T(1024)S(1)} %copy-done.33), kind=kOutput, calls=%fused_computation.25 | convolution fusion | flops 4836556800 | bytes 17312768 | tf_op jit(solution)/shard_map/dot_general | solution.py:801
  198.6 86.9 %mixer_backward.1 = (bf16[2048,1920]{1,0:T(8,128)(2,1)}, f32[8,1024]{1,0:T(8,128)}, f32[8,768]{1,0:T(8,128)}, f32[8,128]{1,0:T(8,128)}, f32[192,768]{1,0:T(8,128)}) custom-call(f32[2048,1920]{1,0:T(8,128)} %fusion.7.pre_ref, f32[2048,1024]{1,0:T(8,128)} %get-tuple-element.55.conv_ref, f32[2048,768]{1,0:T(8,128)} %get-tuple-element.56.scanned_ref, ...), custom_call_target="tpu_custom_call" | custom-call | flops 3221225472 | bytes 56623104 | tf_op jit(solution)/shard_map/mixer_backward/pallas_call | solution.py:610
  285.6 18.3 %multiply_reduce_fusion = (f32[1536]{0:T(1024)S(1)}, bf16[2048,1,1536]{2,0,1:T(8,128)(2,1)}) fusion(bf16[2048,1,1536]{2,0,1:T(8,128)(2,1)} %all-gather.3.cloned.1.call-done, bf16[2048,1920]{1,0:T(8,128)(2,1)} %get-tuple-element.59, bf16[1536,2688]{1,0:T(8,128)(2,1)S(1)} %bitcast.54), kind=kOutput, calls=%fused_computation | convolution fusion | flops 12092176384 | bytes 26351616 | tf_op jit(solution)/shard_map/dot_general | solution.py:30
  305.8 20.7 %fusion.5.terms_ref = f32[1536,1920]{1,0:T(8,128)} fusion(bf16[2048,1920]{1,0:T(8,128)(2,1)} %get-tuple-element.59, bf16[2048,1,1536]{2,0,1:T(8,128)(2,1)} %all-gather.3.cloned.1.call-done), kind=kOutput, calls=%fused_computation.7 | convolution fusion | flops 12079595520 | bytes 25952256 | tf_op jit(solution)/shard_map/dot_general | solution.py:801
  326.7 83.4 %sum_dp.1 = (f32[192,1920]{1,0:T(8,128)}, f32[8,2176]{1,0:T(8,128)}, f32[8,2176]{1,0:T(8,128)}, f32[48,256]{1,0:T(8,128)}) custom-call(f32[1536,1920]{1,0:T(8,128)} %fusion.5.terms_ref, f32[8,2176]{1,0:T(8,128)} %pad_maximum_fusion.1.small_ref), custom_call_target="tpu_custom_call" | custom-call | bytes 240000000 | tf_op jit(solution)/shard_map/sum_dp/pallas_call | solution.py:243
  419.6 1.4 multiply_subtract_fusion.4
  421.0 1.5 multiply_subtract_fusion.3
  422.5 1.5 slice_bitcast_fusion.1
  424.1 1.5 multiply_subtract_fusion.1
  425.6 2.5 multiply_subtract_fusion
  428.1 2.7 fusion.22
  430.8 18.6 %reduce-scatter.3.cloned.1.call-done = bf16[512,1,1536]{2,0,1:T(8,128)(2,1)} async-done(((bf16[2048,1,1536]{2,0,1:T(8,128)(2,1)}), bf16[512,1,1536]{2,0,1:T(8,128)(2,1)}) %reduce-scatter.3.cloned.1.call-update) | async-done | bytes 1572880 | tf_op jit(solution)/shard_map/reduce_scatter | solution.py:737
  449.5 4.3 fusion.25
  453.8 4.9 %copy.127 = f32[512,1,1536]{2,1,0:T(1,128)} copy(f32[512,1,1536]{2,0,1:T(8,128)S(1)} %get-tuple-element.259) | data formatting | bytes 6291456
  (163 shorter events, 21.9 us)
Async XLA Ops:
  7.2 98.1 %all-gather.3.cloned.1.call-start = ((), (), s32[]{:S(2)}) async-start(), calls=%async_computation.2 | async-start | bytes 7864320 | tf_op jit(solution)/shard_map/all_gather | solution.py:693
  12.2 144.8 %all-gather.5.cloned.1.call-start = ((), (), s32[]{:S(2)}) async-start(), calls=%async_computation.3 | async-start | bytes 7864320 | tf_op jit(solution)/shard_map/all_gather | solution.py:710
  13.0 415.1 %reduce-scatter.5.cloned.1.call-start = ((), (), s32[]{:S(2)}) async-start(), calls=%async_computation.5 | async-start | bytes 7864320 | tf_op jit(solution)/shard_map/reduce_scatter | solution.py:746
  26.2 77.6 %copy-start.18 = (f32[5,768]{1,0:T(8,128)S(1)}, f32[5,768]{1,0:T(8,128)}, u32[]{:S(2)}) copy-start(f32[5,768]{1,0:T(8,128)} %param.35) | copy-start | bytes 46084
  26.2 77.6 %copy-start.26 = (f32[5,256]{1,0:T(8,128)S(1)}, f32[5,256]{1,0:T(8,128)}, u32[]{:S(2)}) copy-start(f32[5,256]{1,0:T(8,128)} %param.36) | copy-start | bytes 15364
  187.1 98.4 %slice-start = ((s8[8257536]{0:T(1024)(128)(4,1)}), s8[4194304]{0:T(1024)(128)(4,1)S(1)}, s32[]{:S(2)}) async-start(s8[8257536]{0:T(1024)(128)(4,1)} %bitcast.53), calls=%async_computation.6 | async-start | bytes 8388608
  198.6 86.9 %slice-start.1 = ((s8[8257536]{0:T(1024)(128)(4,1)}), s8[4063232]{0:T(1024)(128)(4,1)S(1)}, s32[]{:S(2)}) async-start(s8[8257536]{0:T(1024)(128)(4,1)} %bitcast.53), calls=%async_computation.7 | async-start | bytes 8126464
  304.0 145.5 %reduce-scatter.3.cloned.1.call-start = ((), (), s32[]{:S(2)}) async-start(), calls=%async_computation.4 | async-start | bytes 7864320 | tf_op jit(solution)/shard_map/reduce_scatter | solution.py:737
  326.5 89.9 %copy-start.42 = (f32[3,12]{1,0:T(4,128)S(1)}, f32[3,12]{1,0:T(4,128)}, u32[]{:S(2)}) copy-start(f32[3,12]{1,0:T(4,128)} %param.37) | copy-start | bytes 436
  326.5 89.9 %copy-start.46 = (f32[3,12]{1,0:T(4,128)S(1)}, f32[3,12]{1,0:T(4,128)}, u32[]{:S(2)}) copy-start(f32[3,12]{1,0:T(4,128)} %param.46) | copy-start | bytes 436
  326.5 89.9 %copy-start.47 = (f32[3,12]{1,0:T(4,128)S(1)}, f32[3,12]{1,0:T(4,128)}, u32[]{:S(2)}) copy-start(f32[3,12]{1,0:T(4,128)} %param.55) | copy-start | bytes 436
  326.5 90.5 %copy-start.34 = (f32[768]{0:T(1024)S(1)}, f32[768]{0:T(1024)}, u32[]{:S(2)}) copy-start(f32[768]{0:T(1024)} %param.38) | copy-start | bytes 9220
  326.6 90.5 %copy-start.43 = (f32[768]{0:T(1024)S(1)}, f32[768]{0:T(1024)}, u32[]{:S(2)}) copy-start(f32[768]{0:T(1024)} %param.47) | copy-start | bytes 9220
  326.6 90.5 %copy-start.44 = (f32[768]{0:T(1024)S(1)}, f32[768]{0:T(1024)}, u32[]{:S(2)}) copy-start(f32[768]{0:T(1024)} %param.56) | copy-start | bytes 9220
  326.6 91.1 %copy-start.37 = (f32[1536]{0:T(1024)S(1)}, f32[1536]{0:T(1024)}, u32[]{:S(2)}) copy-start(f32[1536]{0:T(1024)} %param.40) | copy-start | bytes 18436
  326.6 91.1 %copy-start.38 = (f32[1536]{0:T(1024)S(1)}, f32[1536]{0:T(1024)}, u32[]{:S(2)}) copy-start(f32[1536]{0:T(1024)} %param.49) | copy-start | bytes 18436
  326.6 91.7 %copy-start.39 = (f32[5,256]{1,0:T(8,128)S(1)}, f32[5,256]{1,0:T(8,128)}, u32[]{:S(2)}) copy-start(f32[5,256]{1,0:T(8,128)} %param.45) | copy-start | bytes 15364
  326.6 91.7 %copy-start.40 = (f32[5,256]{1,0:T(8,128)S(1)}, f32[5,256]{1,0:T(8,128)}, u32[]{:S(2)}) copy-start(f32[5,256]{1,0:T(8,128)} %param.54) | copy-start | bytes 15364
  326.6 93.0 %copy-start.29 = (f32[5,768]{1,0:T(8,128)S(1)}, f32[5,768]{1,0:T(8,128)}, u32[]{:S(2)}) copy-start(f32[5,768]{1,0:T(8,128)} %param.44) | copy-start | bytes 46084
  326.6 93.0 %copy-start.30 = (f32[5,768]{1,0:T(8,128)S(1)}, f32[5,768]{1,0:T(8,128)}, u32[]{:S(2)}) copy-start(f32[5,768]{1,0:T(8,128)} %param.53) | copy-start | bytes 46084
  326.7 94.3 %copy-start.16 = (f32[48,256]{1,0:T(8,128)S(1)}, f32[48,256]{1,0:T(8,128)}, u32[]{:S(2)}) copy-start(f32[48,256]{1,0:T(8,128)} %param.34) | copy-start | bytes 147460
  326.7 94.3 %copy-start.22 = (f32[48,256]{1,0:T(8,128)S(1)}, f32[48,256]{1,0:T(8,128)}, u32[]{:S(2)}) copy-start(f32[48,256]{1,0:T(8,128)} %param.43) | copy-start | bytes 147460
  326.7 94.3 %copy-start.23 = (f32[48,256]{1,0:T(8,128)S(1)}, f32[48,256]{1,0:T(8,128)}, u32[]{:S(2)}) copy-start(f32[48,256]{1,0:T(8,128)} %param.52) | copy-start | bytes 147460
  428.1 21.4 %copy-start.1 = (bf16[512,1,1536]{2,0,1:T(8,128)(2,1)S(1)}, bf16[512,1,1536]{2,0,1:T(8,128)(2,1)}, u32[]{:S(2)}) copy-start(bf16[512,1,1536]{2,0,1:T(8,128)(2,1)} %param.30) | copy-start | bytes 4718596
  (30 other events, 176.2 us)
Sparse Core Ops, SparseCore 0:
  12.4 72.7 all-gather.2
  87.0 70.0 all-gather.4
  304.0 67.4 reduce-scatter.4
  374.3 75.0 reduce-scatter.2

commit v3 on v2

--- a/solution.py
+++ b/solution.py
@@ -43,6 +43,7 @@
 
 
 MESH = pl.DeviceIdType.MESH
+LOADS = 8
 
 
 def meet(peers, beside=()):
@@ -121,8 +122,11 @@
 
 
 class Exchange:
-    def __init__(self, n, terms, near_buf, out_buf, far_buf, near_send, near_recv, far_send, far_recv):
-        self.n, self.terms, self.near_buf, self.out_buf, self.far_buf = n, terms, near_buf, out_buf, far_buf
+    def __init__(
+        self, n, terms, own_buf, near_buf, out_buf, far_buf, own_sem, near_send, near_recv, far_send, far_recv
+    ):
+        self.n, self.terms, self.own_buf, self.own_sem = n, terms, own_buf, own_sem
+        self.near_buf, self.out_buf, self.far_buf = near_buf, out_buf, far_buf
         self.near_send, self.near_recv, self.far_send, self.far_recv = near_send, near_recv, far_send, far_recv
         self.chips = n // 2
         self.rows = terms.shape[0] // n
@@ -132,12 +136,16 @@
         self.order = [lax.rem(me // 2 + 1 + k, self.chips) for k in range(self.chips)]
 
     def block(self, index):
-        return pl.ds(pl.multiple_of(index * self.rows, self.rows), self.rows)
+        return self.terms.at[pl.ds(pl.multiple_of(index * self.rows, self.rows), self.rows), :]
+
+    def kept(self, k):
+        return pltpu.make_async_copy(
+            self.block(2 * self.order[k] + self.core), self.own_buf.at[k], self.own_sem.at[k]
+        )
 
     def near(self, k):
-        index = 2 * self.order[k] + 1 - self.core
         return send(
-            self.terms.at[self.block(index), :], self.near_buf.at[k],
+            self.block(2 * self.order[k] + 1 - self.core), self.near_buf.at[k],
             self.near_send.at[k], self.near_recv.at[k], self.partner,
         )
 
@@ -147,21 +155,20 @@
             self.far_send.at[k], self.far_recv.at[k], 2 * self.order[k] + self.core,
         )
 
-    def start(self):
-        for k in range(self.chips):
-            self.near(k).start()
+    def start_one(self, k):
+        self.kept(k).start()
+        self.near(k).start()
 
     def pair_sum(self, k):
-        return self.terms[self.block(2 * self.order[k] + self.core), :] + self.near_buf[k]
-
-    def forward(self):
-        for k in range(self.chips - 1):
-            self.near(k).wait()
-            self.out_buf[k] = self.pair_sum(k).astype(bf16)
-            self.far(k).start()
+        self.kept(k).wait()
+        self.near(k).wait()
+        return self.own_buf[k] + self.near_buf[k]
+
+    def forward_one(self, k):
+        self.out_buf[k] = self.pair_sum(k).astype(bf16)
+        self.far(k).start()
 
     def finish(self):
-        self.near(self.chips - 1).wait()
         total = self.pair_sum(self.chips - 1)
         for k in range(self.chips - 1):
             self.far(k).wait()
@@ -173,8 +180,10 @@
         chips = n // 2
         return [
             pltpu.VMEM((chips, rows, cols), f32),
+            pltpu.VMEM((chips, rows, cols), f32),
             pltpu.VMEM((chips - 1, rows, cols), bf16),
             pltpu.VMEM((chips - 1, rows, cols), bf16),
+            pltpu.SemaphoreType.DMA((chips,)),
             pltpu.SemaphoreType.DMA((chips,)),
             pltpu.SemaphoreType.DMA((chips,)),
             pltpu.SemaphoreType.DMA((chips - 1,)),
@@ -188,84 +197,150 @@
 
 
 def sum_kernel(
-    n, shards, start, terms_ref, small_ref, own_ref, small_out_ref, shared_ref, state_ref, *scratch
+    n, shards, wide, states, left_hbm, right_hbm, small_ref,
+    inner_ref, step_ref, state_ref, taps_ref, wide_ref, head_ref, state_taps_ref, gain_ref,
+    left_ref, right_ref, load_sems,
+    pair, near_buf, out_buf, far_buf, small_sum, small_buf, state_out, state_buf, shared_buf,
+    near_send, near_recv, far_send, far_recv, small_send, small_recv,
+    state_send, state_recv, shared_send, shared_recv,
 ):
-    small_buf, small_send, small_recv, state_out, state_buf, shared_buf = scratch[7:13]
-    state_send, state_recv, shared_send, shared_recv = scratch[13:]
+    rows, _ = pair.shape[2:]
+    chips = n // 2
+    loads = []
+    for source, target, base in ((right_hbm, right_ref, 0), (left_hbm, left_ref, LOADS)):
+        piece = source.shape[0] // LOADS
+        for k in range(LOADS):
+            part = pl.ds(k * piece, piece)
+            loads.append(pltpu.make_async_copy(source.at[part, :], target.at[part, :], load_sems.at[base + k]))
+    for load in loads:
+        load.start()
+    me = lax.axis_index("dp")
+    core = lax.rem(me, 2)
+    partner = me + 1 - 2 * core
     others = all_others(n)
     beside = all_others(shards, "tensor")
     meet(others, beside)
-    exchange = Exchange(n, terms_ref, *scratch[:7])
-    exchange.start()
     copies = [
         send(small_ref, small_buf.at[k], small_send.at[k], small_recv.at[k], others[k])
         for k in range(n - 1)
     ]
     for copy in copies:
         copy.start()
-    exchange.forward()
+
+    def chip_of(k):
+        return lax.rem(me // 2 + 1 + k, chips)
+
+    def near(k):
+        return send(pair.at[k, 1 - core], near_buf.at[k], near_send.at[k], near_recv.at[k], partner)
+
+    def far(k):
+        return send(
+            out_buf.at[k], far_buf.at[k], far_send.at[k], far_recv.at[k], 2 * chip_of(k) + core
+        )
+
+    def product(k):
+        start = pl.multiple_of(chip_of(k) * 2 * rows, 2 * rows)
+        both = mm(left_ref[pl.ds(start, 2 * rows), :], right_ref[...])
+        pair[k, 0] = both[:rows]
+        pair[k, 1] = both[rows:]
+        near(k).start()
+
+    def step(k, carry):
+        product(k + 1)
+        near(k).wait()
+        out_buf[k] = (pair[k, core] + near_buf[k]).astype(bf16)
+        far(k).start()
+        return carry
+
+    for load in loads:
+        load.wait()
+    product(0)
+    lax.fori_loop(0, chips - 1, step, 0)
     small = small_ref[...]
     for k in range(n - 1):
         copies[k].wait()
         small = small + small_buf[k]
-    small_out_ref[...] = small
-    own_ref[...] = exchange.finish()
-    rows, cols = state_ref.shape
-    for k in range(shards):
-        state_out[k] = own_ref[k * rows : (k + 1) * rows, start : start + cols]
+    small_sum[...] = small
     shared = [
-        send(small_out_ref, shared_buf.at[k], shared_send.at[k], shared_recv.at[k], beside[k], "tensor")
+        send(small_sum, shared_buf.at[k], shared_send.at[k], shared_recv.at[k], beside[k], "tensor")
         for k in range(shards - 1)
     ]
+    for copy in shared:
+        copy.start()
+    taps = taps_ref.shape[0]
+    taps_ref[...] = small[:taps, :wide]
+    wide_ref[...] = small[0:1, wide + states : 2 * wide + states]
+    head_ref[...] = small[:, 2 * wide + states : 2 * wide + states + LANES]
+    for k in range(shards - 1):
+        shared[k].wait()
+        small = small + shared_buf[k]
+    state_taps_ref[...] = small[:taps, wide : wide + states]
+    gain_ref[...] = small[:, 2 * wide + states + LANES :]
+    near(chips - 1).wait()
+    total = pair[chips - 1, core] + near_buf[chips - 1]
+    for k in range(chips - 1):
+        far(k).wait()
+        total = total + far_buf[k].astype(f32)
+    part_rows = state_ref.shape[0]
+    for k in range(shards):
+        state_out[k] = total[k * part_rows : (k + 1) * part_rows, 2 * wide : 2 * wide + states]
     parts = [
         send(
             state_out.at[beside[k]], state_buf.at[k], state_send.at[k], state_recv.at[k], beside[k], "tensor"
         )
         for k in range(shards - 1)
     ]
-    for copy in shared + parts:
+    for copy in parts:
         copy.start()
-    total = state_out[lax.axis_index("tensor")]
-    for k in range(shards - 1):
-        shared[k].wait()
-        small = small + shared_buf[k]
-    shared_ref[...] = small
+    inner_ref[0] = total[:, :wide]
+    inner_ref[1] = total[:, wide : 2 * wide]
+    step_ref[...] = total[:, 2 * wide + states :]
+    mine = state_out[lax.axis_index("tensor")]
     for k in range(shards - 1):
         parts[k].wait()
-        total = total + state_buf[k]
-    state_ref[...] = total
-
-
-def sum_dp(terms, small, n, shards, start, states):
-    rows, cols = terms.shape[0] // n, terms.shape[1]
+        mine = mine + state_buf[k]
+    state_ref[...] = mine
+
+
+def sum_dp(left_t, right, small, n, shards, wide, states, taps):
+    rows, cols = left_t.shape[0] // n, right.shape[1]
+    chips = n // 2
     part = (rows // shards, states)
+    gain_cols = small.shape[1] - 2 * wide - states - LANES
     vmem = pl.BlockSpec(memory_space=pltpu.VMEM)
+    shapes = [
+        (2, rows, wide), (rows, cols - 2 * wide - states), part, (taps, wide), (1, wide),
+        (8, LANES), (taps, states), (8, gain_cols),
+    ]
+    dma = pltpu.SemaphoreType.DMA
     return pl.pallas_call(
-        functools.partial(sum_kernel, n, shards, start),
-        out_shape=[
-            jax.ShapeDtypeStruct((rows, cols), f32),
-            jax.ShapeDtypeStruct(small.shape, f32),
-            jax.ShapeDtypeStruct(small.shape, f32),
-            jax.ShapeDtypeStruct(part, f32),
-        ],
-        in_specs=[vmem, vmem],
-        out_specs=[vmem, vmem, vmem, vmem],
-        scratch_shapes=Exchange.scratch(n, rows, cols)
-        + [
+        functools.partial(sum_kernel, n, shards, wide, states),
+        out_shape=[jax.ShapeDtypeStruct(shape, f32) for shape in shapes],
+        in_specs=[pl.BlockSpec(memory_space=pl.ANY)] * 2 + [vmem],
+        out_specs=[vmem] * len(shapes),
+        scratch_shapes=[
+            pltpu.VMEM(left_t.shape, bf16),
+            pltpu.VMEM(right.shape, bf16),
+            dma((2 * LOADS,)),
+            pltpu.VMEM((chips, 2, rows, cols), f32),
+            pltpu.VMEM((chips, rows, cols), f32),
+            pltpu.VMEM((chips - 1, rows, cols), bf16),
+            pltpu.VMEM((chips - 1, rows, cols), bf16),
+            pltpu.VMEM(small.shape, f32),
             pltpu.VMEM((n - 1,) + small.shape, f32),
-            pltpu.SemaphoreType.DMA((n - 1,)),
-            pltpu.SemaphoreType.DMA((n - 1,)),
             pltpu.VMEM((shards,) + part, f32),
             pltpu.VMEM((shards - 1,) + part, f32),
             pltpu.VMEM((shards - 1,) + small.shape, f32),
+            dma((chips,)), dma((chips,)), dma((chips - 1,)), dma((chips - 1,)),
+            dma((n - 1,)), dma((n - 1,)),
         ]
-        + [pltpu.SemaphoreType.DMA((shards - 1,))] * 4,
+        + [dma((shards - 1,))] * 4,
         compiler_params=pltpu.CompilerParams(
-            collective_id=1, has_side_effects=True, vmem_limit_bytes=56 * 1024 * 1024
+            collective_id=1, has_side_effects=True, vmem_limit_bytes=60 * 1024 * 1024
         ),
         cost_estimate=pl.CostEstimate(flops=0, bytes_accessed=240_000_000, transcendentals=0),
         name="sum_dp",
-    )(terms, small)
+    )(left_t, right, small)
 
 
 def token_kernel(shards, own_ref, total_ref, buf, send_sem, recv_sem):
@@ -389,24 +464,31 @@
 
 
 def backward_kernel(
-    n, width, size, pre_ref, conv_ref, scanned_ref, dnormed_ref, token_ref, states_ref,
+    n, blocks, width, size, pre_ref, conv_ref, scanned_ref, dnormed_ref, token_ref, states_ref,
     taps_ref, heads_ref, skip_ref, gain_ref, spread_ref, gather_ref, terms_ref,
     dpre_ref, taps_grad_ref, wide_grad_ref, heads_grad_ref, own_ref,
     ext, dstate, dscores, in_rows, out_rows, dstate_b, finals, *scratch,
 ):
     exchange = Exchange(n, terms_ref, *scratch)
     opening = (pl.program_id(0) == 0) & (pl.program_id(1) == 0)
-    middle = (pl.program_id(0) == 0) & (pl.program_id(1) == 1)
     closing = (pl.program_id(0) == pl.num_programs(0) - 1) & (pl.program_id(1) == pl.num_programs(1) - 1)
 
     @pl.when(opening)
     def _():
         meet(all_others(n))
-        exchange.start()
-
-    @pl.when(middle)
-    def _():
-        exchange.forward()
+
+    far_steps = [1 + k * (blocks - 2) // (exchange.chips - 1) for k in range(exchange.chips - 1)]
+    near_steps = [step - 1 for step in far_steps] + [blocks - 2]
+    for step in range(blocks - 1):
+        fars = [k for k in range(exchange.chips - 1) if far_steps[k] == step]
+        nears = [k for k in range(exchange.chips) if near_steps[k] == step]
+
+        @pl.when((pl.program_id(0) == 0) & (pl.program_id(1) == step))
+        def _(fars=fars, nears=nears):
+            for k in fars:
+                exchange.forward_one(k)
+            for k in nears:
+                exchange.start_one(k)
 
     count = pre_ref.shape[0]
     half = count // 2
@@ -555,6 +637,8 @@
     @pl.when(closing)
     def _():
         own_ref[...] = exchange.finish()
+        skips = jnp.broadcast_to(wide_grad_ref[1:2, :], (CARRY, width))
+        heads_grad_ref[2:3, :] = mm_split(skips, gather_ref[...])[0:1]
 
 
 def whole(shape):
@@ -608,14 +692,14 @@
         return pl.BlockSpec((count, cols), lambda s, i: (s * blocks + blocks - 1 - i, 0))
 
     return pl.pallas_call(
-        functools.partial(backward_kernel, n, width, size),
+        functools.partial(backward_kernel, n, blocks, width, size),
         grid=(seqs, blocks),
         in_specs=[
             block(cat), block(conv_width), block(width), block(width), block(2),
             pl.BlockSpec((1, state_size, width), lambda s, i: (s * blocks + blocks - 1 - i, 0, 0)),
             whole(taps.shape), whole(heads.shape), whole(skip.shape), whole(gain.shape),
             whole(spread.shape), whole(gather.shape),
-            pl.BlockSpec(memory_space=pltpu.VMEM),
+            pl.BlockSpec(memory_space=pl.ANY),
         ],
         out_specs=[
             block(cat), whole((8, conv_width)), whole((8, width)), whole((8, LANES)),
@@ -757,35 +841,25 @@
         ],
         axis=1,
     )
-    grad_own, small_sums, shared_sums, grad_state = sum_dp(
-        contract_first(flat_in, d_pre), small, replicas, shards, 2 * wide, states
-    )
-    taps_grad = small_sums[:, : wide + states]
-    wide_grad = small_sums[:, wide + states : 2 * wide + states]
-    head_grad = small_sums[:, 2 * wide + states : 2 * wide + states + LANES]
-    grad_gain_rows = shared_sums[:, 2 * wide + states + LANES :].reshape(-1)[:features]
+    grad_inner, step_sums, grad_state, grad_taps, grad_wide, head_sums, grad_state_taps, gain_sums = sum_dp(
+        flat_in.T, d_pre, small, replicas, shards, wide, states, inner_taps.shape[0]
+    )
+    grad_output = grad_output_t.T
 
     d_hat = d_in * input_gain
     gradient_hidden = cotangent.astype(f32) + rstd * (
         d_hat - normed * jnp.mean(d_hat * normed, -1, keepdims=True)
     )
-    grad_skip = jnp.sum(wide_grad[1].reshape(heads, size), axis=1)
-    split_terms = (
-        taps_grad[: inner_taps.shape[0], :wide],
-        jnp.concatenate([head_grad[:2, :heads], grad_skip[None]], axis=0),
-        wide_grad[0],
-    )
-    own = grad_own
     grads = (
-        grad_gain_rows,
-        jnp.stack([own[:, :wide], own[:, wide : 2 * wide]]),
-        own[:, 2 * wide + states : 2 * wide + states + heads],
+        gain_sums.reshape(-1)[:features],
+        grad_inner,
+        step_sums[:, :heads],
         grad_state,
-        split_terms[0],
-        shared_sums[: state_taps.shape[0], wide : wide + states],
-        split_terms[1],
-        split_terms[2],
-        grad_output_t.T,
+        grad_taps,
+        grad_state_taps,
+        head_sums[:3, :heads],
+        grad_wide[0],
+        grad_output,
     )
     stepped = [
         adam_step(param, first, second_moment, grad, rate)

time: 476 us -> 494 us (1.038)
  waiting for transfers between devices: 23.5 us -> 50.1 us
  local copies, waits for them, and re-layouts: 17.5 us -> 31.2 us
  Pallas kernels: 282 us -> 269 us
  matrix products: 90.8 us -> 79.1 us
    reduce_scatter x1, waiting for transfers between devices: 18.6 us -> 45.2 us  [body(): lax.psum_scatter(branch_part, 'tensor', scatter_dimension=0, tiled=True)]
    unnamed x113 -> x89, local copies, waits for them, and re-layouts: 10.5 us -> 25.4 us
    pallas_call x2, Pallas kernels: 170 us -> 157 us  [the longest x1 85.8 us: run_backward(): pl.pallas_call(functools.partial(backward_kernel, n, blocks, width, size)...]
    dot_general x2 -> x1, matrix products: 32.2 us -> 20.2 us  [contract_first(): lax.dot_general(left, right, (((0,), (0,)), ((), ())), preferred_element_...]
  transfers between devices with their start and end apart: 4 -> 4, of which waited for: 2 -> 2; matrix products, arithmetic and copies ran while one was open for 14% -> 11% of each run, Pallas kernels for 41% -> 36%
where the time goes in v3:
time: 494 us; the launch traced here: 484 us
  Pallas kernels  269 us (54%)
  matrix products  79.1 us (16%)
  waiting for transfers between devices  50.1 us (10%)
  local copies, waits for them, and re-layouts  31.2 us (6%)
  other arithmetic  30.5 us (6%)
  between operations  14.6 us (3%)
  blocking collectives  9.84 us (2%)
    pallas_call x1, Pallas kernels, run_backward(): pl.pallas_call(functools.partial(backward_kernel, n, blocks, width, size)...  85.8 us
    pallas_call x1, Pallas kernels, gather_dp(): pl.pallas_call(functools.partial(gather_kernel, n), out_shape=jax.ShapeDt...  77 us
    pallas_call x1, Pallas kernels, sum_dp(): pl.pallas_call(functools.partial(sum_kernel, n, shards, wide, states), ou...  70.7 us
    reduce_scatter x1, waiting for transfers between devices, body(): lax.psum_scatter(branch_part, 'tensor', scatter_dimension=0, tiled=True)  45.2 us
    dot_general x2, matrix products, mm(): lax.dot_general(a, b, (((1,), (0,)), ((), ())), preferred_element_type=f32)  29.6 us
    dot_general x2, matrix products, mm_nt(): lax.dot_general(a, b, (((1,), (1,)), ((), ())), preferred_element_type=f32)  29.3 us
    pallas_call x1, Pallas kernels, run_forward(): pl.pallas_call(functools.partial(forward_kernel, width, size), grid=(seqs...  28.9 us
    unnamed x89, local copies, waits for them, and re-layouts  25.4 us
  transfers between devices with their start and end apart: 4, of which 2 were waited for; matrix products, arithmetic and copies ran while one was open for 11% of the time, Pallas kernels for 36%

profile of v3, /device:TPU:0, one launch (start us, length us, event | category | flops | bytes accessed | tf_op | source)
XLA Modules:
  0.0 484.3 jit_solution(14222765014834062096)
XLA Ops:
  7.3 1.7 copy.136
  14.0 9.8 %all_gather.10 = bf16[192,256]{1,0:T(8,128)(2,1)S(1)} all-gather(bf16[48,256]{1,0:T(8,128)(2,1)S(1)} %convert_element_type.68), channel_id=1, replica_groups=mesh['dp'=8,'tensor'=4] {'tensor'}, dimensions={0}, use_global_device_ids=true | all-gather | bytes 122880 | tf_op jit(solution)/shard_map/all_gather | solution.py:776
  25.0 77.0 %gather_dp.1 = bf16[1536,2688]{1,0:T(8,128)(2,1)} custom-call(bf16[192,2688]{1,0:T(8,128)(2,1)} %copy-done.10), custom_call_target="tpu_custom_call" | custom-call | bytes 240000000 | tf_op jit(solution)/shard_map/gather_dp/pallas_call | solution.py:106
  104.2 18.9 %fusion.5.pre_ref = f32[2048,1920]{1,0:T(8,128)} fusion(bf16[2048,1,1536]{0,2,1:T(8,128)(2,1)} %all-gather.3.cloned.1.call-done, bf16[1536,2688]{1,0:T(8,128)(2,1)} %gather_dp.1), kind=kOutput, calls=%fused_computation.7 | convolution fusion | flops 12079595520 | bytes 27918336 | tf_op jit(solution)/shard_map/dot_general | solution.py:26
  123.1 28.9 %mixer_forward.1 = (f32[2048,768]{1,0:T(8,128)}, f32[2048,1024]{1,0:T(8,128)}, f32[2048,768]{1,0:T(8,128)}, f32[8,128,768]{2,1,0:T(8,128)}) custom-call(f32[2048,1920]{1,0:T(8,128)} %fusion.5.pre_ref, f32[5,1024]{1,0:T(8,128)} %copy-done.13, f32[2,128]{1,0:T(2,128)} %select_maximum_fusion.heads_ref, f32[1,768]{1,0:T(1,128)} %broadcast_in_dim_reshape.3.skip_ref, ...), custom_call_target="tpu_custom_call" | custom-call | flops 1610612736 | bytes 40894464 | tf_op jit(solution)/shard_map/mixer_forward/pallas_call | solution.py:658
  152.1 3.7 all-gather.5.cloned.1.call-done
  155.8 10.7 %multiply_reduce_fusion.2 = (f32[2048]{0:T(1024)S(1)}, f32[2048]{0:T(1024)S(1)}, f32[2048,768]{1,0:T(8,128)}) fusion(f32[2048,768]{1,0:T(8,128)} %get-tuple-element.57, f32[768]{0:T(1024)S(1)} %copy-done.27, bf16[1536,2688]{1,0:T(8,128)(2,1)} %gather_dp.1, bf16[2048,1,1536]{2,0,1:T(8,128)(2,1)} %all-gather.5.cloned.1.call-done), kind=kOutput, calls=%fused_computation.12 | convolution fusion | flops 4839698432 | bytes 21253120 | tf_op jit(solution)/shard_map/dot_general | solution.py:26
  167.1 6.2 %sum_tensor.1 = f32[2,2048]{1,0:T(2,128)} custom-call(f32[2,2048]{1,0:T(2,128)} %pad_maximum_fusion.1.own_ref), custom_call_target="tpu_custom_call" | custom-call | tf_op jit(solution)/shard_map/sum_tensor/pallas_call | solution.py:364
  174.1 10.3 %fusion = bf16[2048,1,1536]{0,2,1:T(8,128)(2,1)} fusion(bf16[1536,2688]{1,0:T(8,128)(2,1)} %gather_dp.1, f32[2048,768]{1,0:T(8,128)} %get-tuple-element.57, f32[2048]{0:T(1024)S(1)} %bitcast.52, f32[768]{0:T(1024)S(1)} %copy-done.27), kind=kOutput, calls=%fused_computation.2 | convolution fusion | flops 4839702528 | bytes 14953472 | tf_op jit(solution)/shard_map/dot_general | solution.py:30
  185.7 20.2 %fusion.16.terms_ref = f32[1536,768]{1,0:T(8,128)} fusion(bf16[2048,1,1536]{2,0,1:T(8,128)(2,1)} %all-gather.5.cloned.1.call-done, f32[2048,768]{1,0:T(8,128)} %get-tuple-element.57, f32[2048]{0:T(1024)S(1)} %bitcast.54, f32[768]{0:T(1024)S(1)} %copy-done.27), kind=kOutput, calls=%fused_computation.23 | convolution fusion | flops 4836556800 | bytes 17312768 | tf_op jit(solution)/shard_map/dot_general | solution.py:875
  206.0 85.8 %mixer_backward.1 = (bf16[2048,1920]{1,0:T(8,128)(2,1)}, f32[8,1024]{1,0:T(8,128)}, f32[8,768]{1,0:T(8,128)}, f32[8,128]{1,0:T(8,128)}, f32[192,768]{1,0:T(8,128)}) custom-call(f32[2048,1920]{1,0:T(8,128)} %fusion.5.pre_ref, f32[2048,1024]{1,0:T(8,128)} %get-tuple-element.59.conv_ref, f32[2048,768]{1,0:T(8,128)} %get-tuple-element.60.scanned_ref, ...), custom_call_target="tpu_custom_call" | custom-call | flops 3221225472 | bytes 56623104 | tf_op jit(solution)/shard_map/mixer_backward/pallas_call | solution.py:694
  291.8 19.0 %multiply_reduce_fusion = (f32[1536]{0:T(1024)S(1)}, bf16[2048,1,1536]{0,2,1:T(8,128)(2,1)}) fusion(bf16[2048,1,1536]{0,2,1:T(8,128)(2,1)S(1)} %bitcast.50, bf16[2048,1920]{1,0:T(8,128)(2,1)} %get-tuple-element.63.right_hbm, bf16[1536,2688]{1,0:T(8,128)(2,1)} %gather_dp.1), kind=kOutput, calls=%fused_computation | convolution fusion | flops 12092176384 | bytes 26351616 | tf_op jit(solution)/shard_map/dot_general | solution.py:30
  316.2 70.7 %sum_dp.1 = (f32[2,192,768]{2,1,0:T(8,128)}, f32[192,128]{1,0:T(8,128)}, f32[48,256]{1,0:T(8,128)}, f32[5,768]{1,0:T(8,128)}, f32[1,768]{1,0:T(1,128)}, /*index=...) custom-call(bf16[1536,2048]{1,0:T(8,128)(2,1)} %bitcast.48, bf16[2048,1920]{1,0:T(8,128)(2,1)} %get-tuple-element.63.right_hbm, ...), custom_call_target="tpu_custom_call" | custom-call | bytes 240000000 | tf_op jit(solution)/shard_map/sum_dp/pallas_call | solution.py:316
  388.3 1.7 multiply_subtract_fusion.2
  390.1 1.6 copy.153
  391.6 1.6 copy.154
  393.2 1.6 copy.155
  394.8 1.6 copy.152
  405.6 2.9 multiply_subtract_fusion.1
  408.6 2.4 multiply_subtract_fusion
  410.9 2.2 fusion.20
  413.1 45.2 %reduce-scatter.3.cloned.1.call-done = bf16[512,1,1536]{0,2,1:T(8,128)(2,1)} async-done(((bf16[2048,1,1536]{0,2,1:T(8,128)(2,1)}), bf16[512,1,1536]{0,2,1:T(8,128)(2,1)}) %reduce-scatter.3.cloned.1.call-update) | async-done | bytes 1572880 | tf_op jit(solution)/shard_map/reduce_scatter | solution.py:821
  458.3 5.2 %fusion.23 = (f32[512,1,1536]{0,2,1:T(8,128)}, bf16[512,1,1536]{0,2,1:T(8,128)(2,1)}) fusion(bf16[512,1,1536]{0,2,1:T(8,128)(2,1)S(1)} %copy.136, bf16[512,1,1536]{0,2,1:T(8,128)(2,1)S(1)} %copy-done.1, bf16[512,1,1536]{0,2,1:T(8,128)(2,1)} %copy.140, f32[512]{0:T(512)S(1)} %broadcast_multiply_fusion.3, f32[1536]{0:T(1024)S(1)} %copy-done.14, ...), kind=kLoop, calls=%fused_computation.28 | loop fusion | flops 9437184 | bytes 11020288 | tf_op jit(solution)/shard_map/add | solution.py:850
  463.5 8.6 %copy.151 = f32[512,1,1536]{2,1,0:T(1,128)} copy(f32[512,1,1536]{0,2,1:T(8,128)} %get-tuple-element.262) | data formatting | bytes 6291456
  (133 shorter events, 32.1 us)
Async XLA Ops:
  7.2 97.0 %all-gather.3.cloned.1.call-start = ((), (), s32[]{:S(2)}) async-start(), calls=%async_computation.2 | async-start | bytes 7864320 | tf_op jit(solution)/shard_map/all_gather | solution.py:777
  9.5 4.5 copy-start.3
  11.0 12.9 %copy-start.7 = (f32[768,192]{0,1:T(8,128)S(1)}, f32[768,192]{0,1:T(8,128)}, u32[]{:S(2)}) copy-start(f32[768,192]{0,1:T(8,128)} %param.39) | copy-start | bytes 1769476
  11.1 144.7 %all-gather.5.cloned.1.call-start = ((), (), s32[]{:S(2)}) async-start(), calls=%async_computation.3 | async-start | bytes 7864320 | tf_op jit(solution)/shard_map/all_gather | solution.py:794
  11.8 399.1 %reduce-scatter.5.cloned.1.call-start = ((), (), s32[]{:S(2)}) async-start(), calls=%async_computation.5 | async-start | bytes 7864320 | tf_op jit(solution)/shard_map/reduce_scatter | solution.py:830
  25.0 77.6 %copy-start.17 = (f32[5,768]{1,0:T(8,128)S(1)}, f32[5,768]{1,0:T(8,128)}, u32[]{:S(2)}) copy-start(f32[5,768]{1,0:T(8,128)} %param.35) | copy-start | bytes 46084
  25.0 77.6 %copy-start.22 = (f32[5,256]{1,0:T(8,128)S(1)}, f32[5,256]{1,0:T(8,128)}, u32[]{:S(2)}) copy-start(f32[5,256]{1,0:T(8,128)} %param.36) | copy-start | bytes 15364
  102.6 20.5 %copy-start.13 = (f32[5,1024]{1,0:T(8,128)}, f32[5,1024]{1,0:T(8,128)S(1)}, u32[]{:S(2)}) copy-start(f32[5,1024]{1,0:T(8,128)S(1)} %constant_dynamic-update-slice_fusion.1.taps_ref) | copy-start | bytes 61444
  185.7 106.1 %slice-start = ((s8[6291456]{0:T(1024)(128)(4,1)}), s8[4194304]{0:T(1024)(128)(4,1)S(1)}, s32[]{:S(2)}) async-start(s8[6291456]{0:T(1024)(128)(4,1)} %bitcast.49), calls=%async_computation.6 | async-start | bytes 8388608
  206.0 85.8 %slice-start.1 = ((s8[6291456]{0:T(1024)(128)(4,1)}), s8[2097152]{0:T(1024)(128)(4,1)S(1)}, s32[]{:S(2)}) async-start(s8[6291456]{0:T(1024)(128)(4,1)} %bitcast.49), calls=%async_computation.7 | async-start | bytes 4194304
  310.9 147.4 %reduce-scatter.3.cloned.1.call-start = ((), (), s32[]{:S(2)}) async-start(), calls=%async_computation.4 | async-start | bytes 7864320 | tf_op jit(solution)/shard_map/reduce_scatter | solution.py:821
  311.5 4.0 copy-start.21
  311.5 4.0 copy-start.26
  311.5 4.0 copy-start.32
  316.2 89.5 %copy-start.8 = (f32[768,192]{0,1:T(8,128)S(1)}, f32[768,192]{0,1:T(8,128)}, u32[]{:S(2)}) copy-start(f32[768,192]{0,1:T(8,128)} %param.39) | copy-start | bytes 1769476
  386.9 21.6 %copy-start.4 = (f32[2,192,768]{2,1,0:T(8,128)S(1)}, f32[2,192,768]{2,1,0:T(8,128)}, u32[]{:S(2)}) copy-start(f32[2,192,768]{2,1,0:T(8,128)} %param.32) | copy-start | bytes 3538948
  397.1 13.8 %copy-start.28 = (f32[768]{0:T(1024)}, f32[768]{0:T(1024)S(1)}, u32[]{:S(2)}) copy-start(f32[768]{0:T(1024)S(1)} %reduce.2) | copy-start | bytes 9220
  397.1 11.4 %copy-start.5 = (f32[2,192,768]{2,1,0:T(8,128)S(1)}, f32[2,192,768]{2,1,0:T(8,128)}, u32[]{:S(2)}) copy-start(f32[2,192,768]{2,1,0:T(8,128)} %get-tuple-element.312) | copy-start | bytes 3538948
  397.1 11.4 %copy-start.11 = (f32[2,192,768]{2,1,0:T(8,128)S(1)}, f32[2,192,768]{2,1,0:T(8,128)}, u32[]{:S(2)}) copy-start(f32[2,192,768]{2,1,0:T(8,128)} %param.41) | copy-start | bytes 3538948
  397.1 11.4 %copy-start.12 = (f32[2,192,768]{2,1,0:T(8,128)S(1)}, f32[2,192,768]{2,1,0:T(8,128)}, u32[]{:S(2)}) copy-start(f32[2,192,768]{2,1,0:T(8,128)} %param.50) | copy-start | bytes 3538948
  410.9 47.4 %copy-start.1 = (bf16[512,1,1536]{0,2,1:T(8,128)(2,1)S(1)}, bf16[512,1,1536]{0,2,1:T(8,128)(2,1)}, u32[]{:S(2)}) copy-start(bf16[512,1,1536]{0,2,1:T(8,128)(2,1)} %reduce-scatter.5.cloned.1.call-done) | copy-start | bytes 4718596
  463.5 8.6 %copy-start.2 = (bf16[512,1,1536]{0,2,1:T(8,128)(2,1)S(1)}, bf16[512,1,1536]{0,2,1:T(8,128)(2,1)}, u32[]{:S(2)}) copy-start(bf16[512,1,1536]{0,2,1:T(8,128)(2,1)} %get-tuple-element.263) | copy-start | bytes 4718596
  472.1 3.9 copy-start.23
  472.1 4.4 copy-start.9
  (15 other events, 38.0 us)
Sparse Core Ops, SparseCore 0:
  11.2 72.6 all-gather.2
  85.7 70.0 all-gather.4
  311.0 70.2 reduce-scatter.4
  384.1 74.1 reduce-scatter.2

commit v4 on v3

--- a/solution.py
+++ b/solution.py
@@ -66,55 +66,102 @@
     )
 
 
-def gather_kernel(n, own_ref, full_ref, own_sem, far_send, far_recv, near_send, near_recv):
+def gather_kernel(
+    n, own_ref, full_ref, own_sem, right_send, right_recv, left_send, left_recv, near_send, near_recv
+):
     rows = own_ref.shape[0]
     chips = n // 2
     me = lax.axis_index("dp")
     core = lax.rem(me, 2)
     chip = me // 2
     partner = me + 1 - 2 * core
-    others = [2 * lax.rem(chip + 1 + k, chips) + core for k in range(chips - 1)]
-    meet(others + [partner])
+    meet([2 * lax.rem(chip + 1 + k, chips) + core for k in range(chips - 1)] + [partner])
 
     def place(index):
         return full_ref.at[pl.ds(pl.multiple_of(index * rows, rows), rows), :]
 
-    far = [
-        send(own_ref, place(me), far_send.at[k], far_recv.at[k], others[k]) for k in range(chips - 1)
-    ]
-    for copy in far:
-        copy.start()
-    near = [send(own_ref, place(me), near_send.at[chips - 1], near_recv.at[chips - 1], partner)]
-    near[0].start()
+    def right(k):
+        source = me - 2 * k
+        return send(
+            own_ref if k == 0 else place(source), place(source), right_send.at[k], right_recv.at[k],
+            lax.rem(me + 2, n),
+        )
+
+    def left(k):
+        source = me + 2 * k
+        return send(
+            own_ref if k == 0 else place(source), place(source), left_send.at[k], left_recv.at[k],
+            lax.rem(me + n - 2, n),
+        )
+
+    def near(source, k):
+        return send(
+            own_ref if k == 0 else place(source), place(source), near_send.at[k], near_recv.at[k], partner
+        )
+
+    def sends_right(k):
+        return (chip >= k) & (chip < chips - 1)
+
+    def sends_left(k):
+        return (chip + k < chips) & (chip > 0)
+
     kept = pltpu.make_async_copy(own_ref, place(me), own_sem)
-    kept.start()
     for k in range(chips - 1):
-        source = 2 * lax.rem(chip + chips - 1 - k, chips) + core
-        far[k].wait_recv()
-        copy = send(place(source), place(source), near_send.at[k], near_recv.at[k], partner)
-        copy.start()
-        near.append(copy)
+
+        @pl.when(sends_right(k))
+        def _():
+            right(k).start()
+
+        @pl.when(sends_left(k))
+        def _():
+            left(k).start()
+
+        if k == 0:
+            near(me, 0).start()
+            kept.start()
+
+        @pl.when(chip >= k + 1)
+        def _():
+            right(k).wait_recv()
+            near(me - 2 * (k + 1), 1 + k).start()
+
+        @pl.when(chip + k + 1 < chips)
+        def _():
+            left(k).wait_recv()
+            near(me + 2 * (k + 1), chips + k).start()
+
     kept.wait()
-    for copy in far:
-        copy.wait_send()
-    for copy in near:
-        copy.wait()
+    near(me, 0).wait()
+    for k in range(chips - 1):
+
+        @pl.when(sends_right(k))
+        def _():
+            right(k).wait_send()
+
+        @pl.when(sends_left(k))
+        def _():
+            left(k).wait_send()
+
+        @pl.when(chip >= k + 1)
+        def _():
+            near(me - 2 * (k + 1), 1 + k).wait()
+
+        @pl.when(chip + k + 1 < chips)
+        def _():
+            near(me + 2 * (k + 1), chips + k).wait()
 
 
 def gather_dp(own, n):
     rows, cols = own.shape
+    hops = n // 2 - 1
     return pl.pallas_call(
         functools.partial(gather_kernel, n),
         out_shape=jax.ShapeDtypeStruct((rows * n, cols), own.dtype),
         in_specs=[pl.BlockSpec(memory_space=pltpu.VMEM)],
         out_specs=pl.BlockSpec(memory_space=pl.ANY),
-        scratch_shapes=[
-            pltpu.SemaphoreType.DMA(()),
-            pltpu.SemaphoreType.DMA((n // 2 - 1,)),
-            pltpu.SemaphoreType.DMA((n // 2 - 1,)),
-            pltpu.SemaphoreType.DMA((n // 2,)),
-            pltpu.SemaphoreType.DMA((n // 2,)),
-        ],
+        scratch_shapes=[pltpu.SemaphoreType.DMA(())]
+        + [pltpu.SemaphoreType.DMA((hops,))] * 4
+        + [pltpu.SemaphoreType.DMA((2 * hops + 1,))] * 2,
         compiler_params=pltpu.CompilerParams(collective_id=0, has_side_effects=True),
         cost_estimate=pl.CostEstimate(flops=0, bytes_accessed=240_000_000, transcendentals=0),
         name="gather_dp",
@@ -246,16 +293,19 @@
         near(k).start()
 
     def step(k, carry):
-        product(k + 1)
-        near(k).wait()
-        out_buf[k] = (pair[k, core] + near_buf[k]).astype(bf16)
-        far(k).start()
+        product(k)
+
+        @pl.when(k > 0)
+        def _():
+            near(k - 1).wait()
+            out_buf[k - 1] = (pair[k - 1, core] + near_buf[k - 1]).astype(bf16)
+            far(k - 1).start()
+
         return carry
 
     for load in loads:
         load.wait()
-    product(0)
-    lax.fori_loop(0, chips - 1, step, 0)
+    lax.fori_loop(0, chips, step, 0)
     small = small_ref[...]
     for k in range(n - 1):
         copies[k].wait()
@@ -294,7 +344,8 @@
         copy.start()
     inner_ref[0] = total[:, :wide]
     inner_ref[1] = total[:, wide : 2 * wide]
-    step_ref[...] = total[:, 2 * wide + states :]
+    spare = jnp.zeros((-rows % LANES, LANES), f32)
+    step_ref[...] = jnp.concatenate([total[:, 2 * wide + states :], spare], axis=0).T[:, :rows]
     mine = state_out[lax.axis_index("tensor")]
     for k in range(shards - 1):
         parts[k].wait()
@@ -309,7 +360,7 @@
     gain_cols = small.shape[1] - 2 * wide - states - LANES
     vmem = pl.BlockSpec(memory_space=pltpu.VMEM)
     shapes = [
-        (2, rows, wide), (rows, cols - 2 * wide - states), part, (taps, wide), (1, wide),
+        (2, rows, wide), (LANES, rows), part, (taps, wide), (1, wide),
         (8, LANES), (taps, states), (8, gain_cols),
     ]
     dma = pltpu.SemaphoreType.DMA
@@ -373,6 +424,37 @@
         ],
         compiler_params=pltpu.CompilerParams(collective_id=3, has_side_effects=True),
         name="sum_tensor",
+    )(own)
+
+
+def spread_kernel(shards, own_ref, full_ref, send_sem, recv_sem):
+    beside = all_others(shards, "tensor")
+    me = lax.axis_index("tensor")
+    meet((), beside)
+    copies = [
+        send(own_ref, full_ref.at[me], send_sem.at[k], recv_sem.at[k], beside[k], "tensor")
+        for k in range(shards - 1)
+    ]
+    for copy in copies:
+        copy.start()
+    full_ref[me] = own_ref[...]
+    for copy in copies:
+        copy.wait()
+
+
+def gather_tensor(own, shards):
+    vmem = pl.BlockSpec(memory_space=pltpu.VMEM)
+    return pl.pallas_call(
+        functools.partial(spread_kernel, shards),
+        out_shape=jax.ShapeDtypeStruct((shards,) + own.shape, own.dtype),
+        in_specs=[vmem],
+        out_specs=vmem,
+        scratch_shapes=[
+            pltpu.SemaphoreType.DMA((shards - 1,)),
+            pltpu.SemaphoreType.DMA((shards - 1,)),
+        ],
+        compiler_params=pltpu.CompilerParams(collective_id=4, has_side_effects=True),
+        name="gather_tensor",
     )(own)
 
 
@@ -741,6 +823,10 @@
     return (moved, first_new, second_new)
 
 
+def flip_step(values):
+    return tuple(value.T if k == 2 else value for k, value in enumerate(values))
+
+
 def body(hidden, cotangent, *arrays):
     params, firsts, seconds = arrays[:9], arrays[9:18], arrays[18:27]
     (
@@ -773,7 +859,7 @@
     def by_position(values):
         return values.reshape(seqs, values.shape[0] // seqs, values.shape[1]).transpose(1, 0, 2)
 
-    state_rows = lax.all_gather(state_weight.astype(bf16), "tensor", axis=0, tiled=True)
+    state_rows = gather_tensor(state_weight.astype(bf16), shards).reshape(-1, states)
     full_in = lax.all_gather(normed_in, "tensor", axis=0, tiled=True)
     weights_own = jnp.concatenate(
         [
@@ -819,7 +905,6 @@
     branch_part = by_position(mm_nt(normed_out, output_t)).astype(bf16)
     branch_part, d_normed = lax.optimization_barrier((branch_part, d_normed))
     branch = lax.psum_scatter(branch_part, "tensor", scatter_dimension=0, tiled=True)
-    result = (base + branch.astype(f32)).astype(bf16)
     output_terms = contract_first(flat_cot, normed_out)
 
     d_pre, taps_grad, wide_grad, head_grad, grad_output_t = run_backward(
@@ -827,9 +912,7 @@
         spread, gather, output_terms, replicas, seqs, GROUP, size,
     )
     d_in_part = mm_nt(d_pre, weights)
-    d_in = lax.psum_scatter(
-        by_position(d_in_part.astype(bf16)), "tensor", scatter_dimension=0, tiled=True
-    ).astype(f32)
+    d_in = lax.psum_scatter(by_position(d_in_part.astype(bf16)), "tensor", scatter_dimension=0, tiled=True).astype(f32)
     grad_gain_rows = jnp.sum(d_in_part * flat_in.astype(f32), axis=0) / input_gain
     gain_cols = -(-features // (8 * LANES)) * LANES
     small = jnp.concatenate(
@@ -846,6 +929,7 @@
     )
     grad_output = grad_output_t.T
 
+    result = (base + branch.astype(f32)).astype(bf16)
     d_hat = d_in * input_gain
     gradient_hidden = cotangent.astype(f32) + rstd * (
         d_hat - normed * jnp.mean(d_hat * normed, -1, keepdims=True)
@@ -853,7 +937,7 @@
     grads = (
         gain_sums.reshape(-1)[:features],
         grad_inner,
-        step_sums[:, :heads],
+        step_sums[:heads],
         grad_state,
         grad_taps,
         grad_state_taps,
@@ -863,8 +947,12 @@
     )
     stepped = [
         adam_step(param, first, second_moment, grad, rate)
-        for param, first, second_moment, grad, rate in zip(params, firsts, seconds, grads, rates)
+        for param, first, second_moment, grad, rate in zip(
+            flip_step(params), flip_step(firsts), flip_step(seconds), grads, rates
+        )
     ]
+    grads = flip_step(grads)
+    stepped = [entry if k != 2 else tuple(value.T for value in entry) for k, entry in enumerate(stepped)]
     moved = [entry[0] for entry in stepped]
     first_new = [entry[1] for entry in stepped]
     second_new = [entry[2] for entry in stepped]

time: 494 us -> 460 us (0.931); the launches traced: 484 us -> 459 us
  blocking collectives: 9.84 us -> 0 us
  waiting for transfers between devices: 50.1 us -> 59 us
  matrix products: 79.1 us -> 70.2 us
  local copies, waits for them, and re-layouts: 31.2 us -> 23.6 us
  Pallas kernels: 269 us -> 262 us
    pallas_call x1, Pallas kernels: 85.8 us -> 70.4 us  [run_backward(): pl.pallas_call(functools.partial(backward_kernel, n, blocks, width, size)...]
    all_gather x1 -> x0, blocking collectives: 9.84 us -> none  [body(): lax.all_gather(state_weight.astype(bf16), 'tensor', axis=0, tiled=True)]
    dot_general x1, matrix products: 20.2 us -> 11 us  [contract_first(): lax.dot_general(left, right, (((0,), (0,)), ((), ())), preferred_element_...]
    reduce_scatter x1, waiting for transfers between devices: 45.2 us -> 53.4 us  [body(): lax.psum_scatter(branch_part, 'tensor', scatter_dimension=0, tiled=True)]
    pallas_call x0 -> x1, Pallas kernels: none -> 7.98 us  [gather_tensor(): pl.pallas_call(functools.partial(spread_kernel, shards), out_shape=jax.Sh...]
    unnamed x89 -> x84, local copies, waits for them, and re-layouts: 25.4 us -> 20 us
    sub x9 -> x8, other arithmetic: 15.5 us -> 13.6 us  [adam_step(): param - rate * (first_hat / (jnp.sqrt(second_hat) + adam_eps) + decay_rat...]
  transfers between devices with their start and end apart: 4 -> 4, of which waited for: 2 -> 2; matrix products, arithmetic and copies ran while one was open for 11% -> 10% of each run, Pallas kernels for 36% -> 40%
where the time goes in v4:
time: 460 us; the launch traced here: 459 us
  Pallas kernels  262 us (57%)
  matrix products  70.2 us (15%)
  waiting for transfers between devices  59 us (13%)
  other arithmetic  30 us (7%)
  local copies, waits for them, and re-layouts  23.6 us (5%)
  between operations  14.2 us (3%)
    pallas_call x1, Pallas kernels, gather_dp(): pl.pallas_call(functools.partial(gather_kernel, n), out_shape=jax.ShapeDt...  77.4 us
    pallas_call x1, Pallas kernels, sum_dp(): pl.pallas_call(functools.partial(sum_kernel, n, shards, wide, states), ou...  70.9 us
    pallas_call x1, Pallas kernels, run_backward(): pl.pallas_call(functools.partial(backward_kernel, n, blocks, width, size)...  70.4 us
    reduce_scatter x1, waiting for transfers between devices, body(): lax.psum_scatter(branch_part, 'tensor', scatter_dimension=0, tiled=True)  53.4 us
    dot_general x2, matrix products, mm(): lax.dot_general(a, b, (((1,), (0,)), ((), ())), preferred_element_type=f32)  29.6 us
    dot_general x2, matrix products, mm_nt(): lax.dot_general(a, b, (((1,), (1,)), ((), ())), preferred_element_type=f32)  29.5 us
    pallas_call x1, Pallas kernels, run_forward(): pl.pallas_call(functools.partial(forward_kernel, width, size), grid=(seqs...  28.9 us
    unnamed x84, local copies, waits for them, and re-layouts  20 us
  transfers between devices with their start and end apart: 4, of which 2 were waited for; matrix products, arithmetic and copies ran while one was open for 10% of the time, Pallas kernels for 40%

profile of v4, /device:TPU:0, one launch (start us, length us, event | category | flops | bytes accessed | tf_op | source)
XLA Modules:
  0.0 459.0 jit_solution(11806445943156452953)
XLA Ops:
  7.3 1.7 copy.103
  9.5 1.6 fusion.19
  13.9 8.0 %gather_tensor.1 = bf16[4,48,256]{2,1,0:T(8,128)(2,1)} custom-call(bf16[48,256]{1,0:T(8,128)(2,1)} %convert_element_type.68.own_ref), custom_call_target="tpu_custom_call" | custom-call | tf_op jit(solution)/shard_map/gather_tensor/pallas_call | solution.py:447
  24.0 77.4 %gather_dp.1 = bf16[1536,2688]{1,0:T(8,128)(2,1)} custom-call(bf16[192,2688]{1,0:T(8,128)(2,1)} %copy-done.10), custom_call_target="tpu_custom_call" | custom-call | bytes 240000000 | tf_op jit(solution)/shard_map/gather_dp/pallas_call | solution.py:157
  103.6 18.9 %fusion.5.pre_ref = f32[2048,1920]{1,0:T(8,128)} fusion(bf16[2048,1,1536]{0,2,1:T(8,128)(2,1)} %all-gather.3.cloned.1.call-done, bf16[1536,2688]{1,0:T(8,128)(2,1)} %gather_dp.1), kind=kOutput, calls=%fused_computation.7 | convolution fusion | flops 12079595520 | bytes 27918336 | tf_op jit(solution)/shard_map/dot_general | solution.py:26
  122.5 28.9 %mixer_forward.1 = (f32[2048,768]{1,0:T(8,128)}, f32[2048,1024]{1,0:T(8,128)}, f32[2048,768]{1,0:T(8,128)}, f32[8,128,768]{2,1,0:T(8,128)}) custom-call(f32[2048,1920]{1,0:T(8,128)} %fusion.5.pre_ref, f32[5,1024]{1,0:T(8,128)} %copy-done.13, f32[2,128]{1,0:T(2,128)} %select_maximum_fusion.heads_ref, f32[1,768]{1,0:T(1,128)} %broadcast_in_dim_reshape.3.skip_ref, ...), custom_call_target="tpu_custom_call" | custom-call | flops 1610612736 | bytes 40894464 | tf_op jit(solution)/shard_map/mixer_forward/pallas_call | solution.py:740
  151.5 4.3 all-gather.5.cloned.1.call-done
  155.8 10.7 %multiply_reduce_fusion.2 = (f32[2048]{0:T(1024)S(1)}, f32[2048]{0:T(1024)S(1)}, f32[2048,768]{1,0:T(8,128)}) fusion(f32[2048,768]{1,0:T(8,128)} %get-tuple-element.57, f32[768]{0:T(1024)S(1)} %copy-done.27, bf16[1536,2688]{1,0:T(8,128)(2,1)} %gather_dp.1, bf16[2048,1,1536]{2,0,1:T(8,128)(2,1)} %all-gather.5.cloned.1.call-done), kind=kOutput, calls=%fused_computation.12 | convolution fusion | flops 4839698432 | bytes 21253120 | tf_op jit(solution)/shard_map/dot_general | solution.py:26
  167.1 6.2 %sum_tensor.1 = f32[2,2048]{1,0:T(2,128)} custom-call(f32[2,2048]{1,0:T(2,128)} %pad_maximum_fusion.1.own_ref), custom_call_target="tpu_custom_call" | custom-call | tf_op jit(solution)/shard_map/sum_tensor/pallas_call | solution.py:415
  174.2 10.3 %fusion = bf16[2048,1,1536]{0,2,1:T(8,128)(2,1)} fusion(bf16[1536,2688]{1,0:T(8,128)(2,1)} %gather_dp.1, f32[2048,768]{1,0:T(8,128)} %get-tuple-element.57, f32[2048]{0:T(1024)S(1)} %bitcast.85, f32[768]{0:T(1024)S(1)} %copy-done.27), kind=kOutput, calls=%fused_computation.2 | convolution fusion | flops 4839702528 | bytes 14953472 | tf_op jit(solution)/shard_map/dot_general | solution.py:30
  185.8 11.0 %fusion.16.terms_ref = f32[1536,768]{1,0:T(8,128)} fusion(bf16[2048,1,1536]{2,0,1:T(8,128)(2,1)} %all-gather.5.cloned.1.call-done, f32[2048,768]{1,0:T(8,128)} %get-tuple-element.57, f32[2048]{0:T(1024)S(1)} %bitcast.87, f32[768]{0:T(1024)S(1)} %copy-done.27), kind=kOutput, calls=%fused_computation.23 | convolution fusion | flops 4836556800 | bytes 17312768 | tf_op jit(solution)/shard_map/dot_general | solution.py:963
  196.9 70.4 %mixer_backward.1 = (bf16[2048,1920]{1,0:T(8,128)(2,1)}, f32[8,1024]{1,0:T(8,128)}, f32[8,768]{1,0:T(8,128)}, f32[8,128]{1,0:T(8,128)}, f32[192,768]{1,0:T(8,128)}) custom-call(f32[2048,1920]{1,0:T(8,128)} %fusion.5.pre_ref, f32[2048,1024]{1,0:T(8,128)} %get-tuple-element.59.conv_ref, f32[2048,768]{1,0:T(8,128)} %get-tuple-element.60.scanned_ref, ...), custom_call_target="tpu_custom_call" | custom-call | flops 3221225472 | bytes 56623104 | tf_op jit(solution)/shard_map/mixer_backward/pallas_call | solution.py:776
  267.3 19.2 %multiply_reduce_fusion = (f32[1536]{0:T(1024)S(1)}, bf16[2048,1,1536]{0,2,1:T(8,128)(2,1)}) fusion(bf16[2048,1,1536]{0,2,1:T(8,128)(2,1)S(1)} %bitcast.82, bf16[2048,1920]{1,0:T(8,128)(2,1)} %get-tuple-element.63.right_hbm, bf16[1536,2688]{1,0:T(8,128)(2,1)} %gather_dp.1), kind=kOutput, calls=%fused_computation | convolution fusion | flops 12092176384 | bytes 26351616 | tf_op jit(solution)/shard_map/dot_general | solution.py:30
  287.9 1.6 copy.107
  290.2 70.9 %sum_dp.1 = (f32[2,192,768]{2,1,0:T(8,128)}, f32[128,192]{1,0:T(8,128)}, f32[48,256]{1,0:T(8,128)}, f32[5,768]{1,0:T(8,128)}, f32[1,768]{1,0:T(1,128)}, /*index=...) custom-call(bf16[1536,2048]{1,0:T(8,128)(2,1)} %bitcast.80, bf16[2048,1920]{1,0:T(8,128)(2,1)} %get-tuple-element.63.right_hbm, ...), custom_call_target="tpu_custom_call" | custom-call | bytes 240000000 | tf_op jit(solution)/shard_map/sum_dp/pallas_call | solution.py:367
  362.7 1.5 multiply_subtract_fusion.7
  371.0 1.5 multiply_subtract_fusion.2
  372.5 2.9 multiply_subtract_fusion.1
  375.4 2.4 multiply_subtract_fusion
  377.8 2.2 fusion.20
  380.0 53.4 %reduce-scatter.3.cloned.1.call-done = bf16[512,1,1536]{0,2,1:T(8,128)(2,1)} async-done(((bf16[2048,1,1536]{0,2,1:T(8,128)(2,1)}), bf16[512,1,1536]{0,2,1:T(8,128)(2,1)}) %reduce-scatter.3.cloned.1.call-update) | async-done | bytes 1572880 | tf_op jit(solution)/shard_map/reduce_scatter | solution.py:907
  433.4 5.2 %fusion.23 = (f32[512,1,1536]{0,2,1:T(8,128)}, bf16[512,1,1536]{0,2,1:T(8,128)(2,1)}) fusion(bf16[512,1,1536]{0,2,1:T(8,128)(2,1)S(1)} %copy.103, bf16[512,1,1536]{0,2,1:T(8,128)(2,1)S(1)} %copy-done.1, bf16[512,1,1536]{0,2,1:T(8,128)(2,1)} %copy.107, f32[512]{0:T(512)S(1)} %broadcast_multiply_fusion, f32[1536]{0:T(1024)S(1)} %copy-done.14, ...), kind=kLoop, calls=%fused_computation.28 | loop fusion | flops 9437184 | bytes 11020288 | tf_op jit(solution)/shard_map/add | solution.py:934
  438.7 8.6 %copy.113 = f32[512,1,1536]{2,1,0:T(1,128)} copy(f32[512,1,1536]{0,2,1:T(8,128)} %get-tuple-element.259) | data formatting | bytes 6291456
  447.3 1.6 copy.112
  (123 shorter events, 24.4 us)
Async XLA Ops:
  7.2 96.4 %all-gather.3.cloned.1.call-start = ((), (), s32[]{:S(2)}) async-start(), calls=%async_computation.2 | async-start | bytes 7864320 | tf_op jit(solution)/shard_map/all_gather | solution.py:863
  9.5 12.5 %copy-start.3 = (f32[2,192,768]{2,1,0:T(8,128)S(1)}, f32[2,192,768]{2,1,0:T(8,128)}, u32[]{:S(2)}) copy-start(f32[2,192,768]{2,1,0:T(8,128)} %param.32) | copy-start | bytes 3538948
  11.0 12.0 %copy-start.7 = (f32[768,192]{0,1:T(8,128)S(1)}, f32[768,192]{0,1:T(8,128)}, u32[]{:S(2)}) copy-start(f32[768,192]{0,1:T(8,128)} %param.39) | copy-start | bytes 1769476
  11.1 144.7 %all-gather.5.cloned.1.call-start = ((), (), s32[]{:S(2)}) async-start(), calls=%async_computation.3 | async-start | bytes 7864320 | tf_op jit(solution)/shard_map/all_gather | solution.py:880
  11.8 366.0 %reduce-scatter.5.cloned.1.call-start = ((), (), s32[]{:S(2)}) async-start(), calls=%async_computation.5 | async-start | bytes 7864320 | tf_op jit(solution)/shard_map/reduce_scatter | solution.py:915
  24.0 78.0 %copy-start.17 = (f32[5,768]{1,0:T(8,128)S(1)}, f32[5,768]{1,0:T(8,128)}, u32[]{:S(2)}) copy-start(f32[5,768]{1,0:T(8,128)} %param.35) | copy-start | bytes 46084
  24.0 78.0 %copy-start.22 = (f32[5,256]{1,0:T(8,128)S(1)}, f32[5,256]{1,0:T(8,128)}, u32[]{:S(2)}) copy-start(f32[5,256]{1,0:T(8,128)} %param.36) | copy-start | bytes 15364
  102.0 20.5 %copy-start.13 = (f32[5,1024]{1,0:T(8,128)}, f32[5,1024]{1,0:T(8,128)S(1)}, u32[]{:S(2)}) copy-start(f32[5,1024]{1,0:T(8,128)S(1)} %constant_dynamic-update-slice_fusion.1.taps_ref) | copy-start | bytes 61444
  185.8 81.5 %slice-start = ((s8[6291456]{0:T(1024)(128)(4,1)}), s8[4194304]{0:T(1024)(128)(4,1)S(1)}, s32[]{:S(2)}) async-start(s8[6291456]{0:T(1024)(128)(4,1)} %bitcast.81), calls=%async_computation.6 | async-start | bytes 8388608
  196.9 70.4 %slice-start.1 = ((s8[6291456]{0:T(1024)(128)(4,1)}), s8[2097152]{0:T(1024)(128)(4,1)S(1)}, s32[]{:S(2)}) async-start(s8[6291456]{0:T(1024)(128)(4,1)} %bitcast.81), calls=%async_computation.7 | async-start | bytes 4194304
  286.5 146.9 %reduce-scatter.3.cloned.1.call-start = ((), (), s32[]{:S(2)}) async-start(), calls=%async_computation.4 | async-start | bytes 7864320 | tf_op jit(solution)/shard_map/reduce_scatter | solution.py:907
  290.2 72.5 %copy-start.31 = (f32[3,12]{1,0:T(4,128)S(1)}, f32[3,12]{1,0:T(4,128)}, u32[]{:S(2)}) copy-start(f32[3,12]{1,0:T(4,128)} %param.37) | copy-start | bytes 436
  290.2 75.3 %copy-start.29 = (f32[5,256]{1,0:T(8,128)S(1)}, f32[5,256]{1,0:T(8,128)}, u32[]{:S(2)}) copy-start(f32[5,256]{1,0:T(8,128)} %param.45) | copy-start | bytes 15364
  290.2 79.4 %copy-start.25 = (f32[5,768]{1,0:T(8,128)S(1)}, f32[5,768]{1,0:T(8,128)}, u32[]{:S(2)}) copy-start(f32[5,768]{1,0:T(8,128)} %param.44) | copy-start | bytes 46084
  290.2 80.8 %copy-start.20 = (f32[48,256]{1,0:T(8,128)S(1)}, f32[48,256]{1,0:T(8,128)}, u32[]{:S(2)}) copy-start(f32[48,256]{1,0:T(8,128)} %param.43) | copy-start | bytes 147460
  290.2 82.3 %copy-start.8 = (f32[768,192]{0,1:T(8,128)S(1)}, f32[768,192]{0,1:T(8,128)}, u32[]{:S(2)}) copy-start(f32[768,192]{0,1:T(8,128)} %param.39) | copy-start | bytes 1769476
  361.2 14.2 %copy-start.4 = (f32[2,192,768]{2,1,0:T(8,128)S(1)}, f32[2,192,768]{2,1,0:T(8,128)}, u32[]{:S(2)}) copy-start(f32[2,192,768]{2,1,0:T(8,128)} %param.32) | copy-start | bytes 3538948
  362.0 15.8 %copy-start.23 = (f32[1536]{0:T(1024)}, f32[1536]{0:T(1024)S(1)}, u32[]{:S(2)}) copy-start(f32[1536]{0:T(1024)S(1)} %slice.51) | copy-start | bytes 18436
  362.7 15.1 %copy-start.28 = (f32[768]{0:T(1024)}, f32[768]{0:T(1024)S(1)}, u32[]{:S(2)}) copy-start(f32[768]{0:T(1024)S(1)} %reduce.2) | copy-start | bytes 9220
  362.7 12.7 %copy-start.5 = (f32[2,192,768]{2,1,0:T(8,128)S(1)}, f32[2,192,768]{2,1,0:T(8,128)}, u32[]{:S(2)}) copy-start(f32[2,192,768]{2,1,0:T(8,128)} %get-tuple-element.310) | copy-start | bytes 3538948
  362.7 12.7 %copy-start.11 = (f32[2,192,768]{2,1,0:T(8,128)S(1)}, f32[2,192,768]{2,1,0:T(8,128)}, u32[]{:S(2)}) copy-start(f32[2,192,768]{2,1,0:T(8,128)} %param.41) | copy-start | bytes 3538948
  362.7 12.7 %copy-start.12 = (f32[2,192,768]{2,1,0:T(8,128)S(1)}, f32[2,192,768]{2,1,0:T(8,128)}, u32[]{:S(2)}) copy-start(f32[2,192,768]{2,1,0:T(8,128)} %param.50) | copy-start | bytes 3538948
  377.8 55.6 %copy-start.1 = (bf16[512,1,1536]{0,2,1:T(8,128)(2,1)S(1)}, bf16[512,1,1536]{0,2,1:T(8,128)(2,1)}, u32[]{:S(2)}) copy-start(bf16[512,1,1536]{0,2,1:T(8,128)(2,1)} %reduce-scatter.5.cloned.1.call-done) | copy-start | bytes 4718596
  438.7 8.6 %copy-start.2 = (bf16[512,1,1536]{0,2,1:T(8,128)(2,1)S(1)}, bf16[512,1,1536]{0,2,1:T(8,128)(2,1)}, u32[]{:S(2)}) copy-start(bf16[512,1,1536]{0,2,1:T(8,128)(2,1)} %get-tuple-element.260) | copy-start | bytes 4718596
  (15 other events, 38.2 us)
Sparse Core Ops, SparseCore 0:
  11.2 72.6 all-gather.2
  85.7 70.0 all-gather.4
  286.6 70.2 reduce-scatter.4
  359.8 73.6 reduce-scatter.2
